TPU v7x, 128 devices: a whole 4x4x4 slice. The times are simulated.
128 devices in a mesh: gx: 4 (over x), gy: 4 (over z_hi, core), gz: 8 (over y, z_lo).
Axes of the slice: x: 4, y: 4, z: 4 (z_hi: 2, z_lo: 2; z = z_hi * 2 + z_lo), core: 2. Of those that a mesh axis runs over, the one named last changes fastest.
Arguments:
- amplitudes: bfloat16 [2, 65536, 2048], P(None, ('gx', 'gy', 'gz')), may hold values from -6 to 6
- pauli_x: int32 [200], replicated, may hold values from 0 to 2047, as said below
- pauli_z: int32 [200], replicated, may hold values from 0 to 2047
- pauli_phase: int32 [200], replicated, may hold values from 0 to 3
Outputs:
- density_real: float32 [2048, 2048], P(('gx', 'gy', 'gz'))
- density_imag: float32 [2048, 2048], P(('gx', 'gy', 'gz'))
- expectations: float32 [2, 200], replicated
Inputs may be any that keep to these rules, and one draw needn't show every extreme that they name: Bit q of the mask acts on kept qubit q (the bit of weight 2^q of the last index); pauli_x and pauli_z of a term are never both zero.
All inputs are finite; a program needn't handle non-finite values.
Results may differ from a plain program's by a relative error of at most 0.0003.
Values sent between devices are 32-bit elements; how exact they have to be, the bound alone decides.
A program may use at most 192 MiB of HBM per device.

v0:
```python
import functools

import jax
import jax.numpy as jnp
from jax import lax
from jax.sharding import Mesh
from jax.sharding import PartitionSpec as P

QUBITS = 11
GY = ("gy_0", "gy_1")
GZ = ("gz_0", "gz_1")
GX_GY_GZ = ("gx", "gy_0", "gy_1", "gz_0", "gz_1")


def in_blocks(array, dim, peers):
    before, after = (array.shape[:dim], array.shape[dim + 1 :])
    return jnp.moveaxis(array.reshape(*before, peers, -1, *after), dim, 0)


def sent_and_summed(array, axis, dim):
    parts = in_blocks(array, dim, lax.axis_size(axis))
    arrived = lax.all_to_all(parts, axis, split_axis=0, concat_axis=0, tiled=True)
    return arrived.sum(axis=0)


def over_axes(array, axes):
    return functools.reduce(lax.psum, axes, array)


def parity_sign(values, masks):
    anded = jnp.bitwise_and(values, masks)
    counted = jnp.zeros_like(anded)
    for bit_index in range(QUBITS):
        counted = counted + jnp.bitwise_and(jnp.right_shift(anded, bit_index), 1)
    return (1 - 2 * jnp.bitwise_and(counted, 1)).astype(jnp.float32)


def phase_parts(pauli_phase):
    phase_real = jnp.where(pauli_phase == 0, 1.0, jnp.where(pauli_phase == 2, -1.0, 0.0)).astype(
        jnp.float32
    )
    phase_imag = jnp.where(pauli_phase == 1, 1.0, jnp.where(pauli_phase == 3, -1.0, 0.0)).astype(
        jnp.float32
    )
    return (phase_real, phase_imag)


def on_device(amplitudes, pauli_x, pauli_z, pauli_phase):
    real_part = amplitudes[0]
    imag_part = amplitudes[1]
    order = real_part.shape[1]
    stacked = jnp.concatenate([real_part, imag_part], 0)
    crossed = jnp.concatenate([imag_part, jnp.negative(real_part)], 0)
    dims = (((0,), (0,)), ((), ()))
    devices = lax.axis_size("gx") * lax.axis_size(GY) * lax.axis_size(GZ)
    own_count = order // devices
    real_rows = lax.dot_general(stacked, stacked, dims, preferred_element_type=jnp.float32)
    imag_rows = lax.dot_general(crossed, stacked, dims, preferred_element_type=jnp.float32)
    by_gx = lax.psum_scatter(
        jnp.concatenate([real_rows, imag_rows], 1), "gx", scatter_dimension=0, tiled=True
    )
    by_gy = lax.psum_scatter(by_gx, GY, scatter_dimension=0, tiled=True)
    summed = sent_and_summed(by_gy, GZ, 0)
    total_cols = amplitudes.shape[1] * devices
    density = summed / total_cols
    density_real = density[:, :order]
    density_imag = density[:, order:]
    first_row = lax.axis_index(GX_GY_GZ) * own_count
    owned_rows = (first_row + jnp.arange(own_count, dtype=jnp.int32))[:, None]
    partner = jnp.bitwise_xor(owned_rows, pauli_x[None, :])
    picked_real = jnp.take_along_axis(density_real, partner, axis=1)
    picked_imag = jnp.take_along_axis(density_imag, partner, axis=1)
    signs = parity_sign(owned_rows, pauli_z[None, :])
    phase_real, phase_imag = phase_parts(pauli_phase)
    sum_real = jnp.sum(signs * picked_real, axis=0)
    sum_imag = jnp.sum(signs * picked_imag, axis=0)
    local_real = phase_real * sum_real - phase_imag * sum_imag
    local_imag = phase_real * sum_imag + phase_imag * sum_real
    expectations = over_axes(jnp.stack([local_real, local_imag], 0), GX_GY_GZ)
    return (density_real, density_imag, expectations)


def solution(mesh):
    finer = Mesh(
        mesh.devices.reshape(mesh.shape["gx"], 2, 2, 4, 2), ("gx", "gy_0", "gy_1", "gz_0", "gz_1")
    )
    in_specs = (P(None, GX_GY_GZ, None), P(), P(), P())
    out_specs = (P(GX_GY_GZ, None), P(GX_GY_GZ, None), P())
    return jax.shard_map(
        on_device, mesh=finer, in_specs=in_specs, out_specs=out_specs, check_vma=False
    )
```

profile of v0, /device:TPU:1, one launch (start us, length us, event | category | flops | bytes accessed | tf_op | source)
XLA Modules:
  0.0 550.7 jit_solution(16060468333758578852)
XLA Ops:
  7.2 0.0 reduce-scatter.3.cloned.1.call-start
  7.2 0.0 copy-start.2
  7.2 1.9 fusion.37
  9.1 0.9 copy-done.2
  10.0 2.5 slice_bitcast_fusion.1
  12.5 12.8 %fusion.4 = f32[2048,2048]{0,1:T(8,128)S(1)} fusion(bf16[512,2048]{1,0:T(8,128)(2,1)} %get-tuple-element.7, bf16[512,2048]{1,0:T(8,128)(2,1)} %get-tuple-element.6), kind=kOutput, calls=%fused_computation.8 | convolution fusion | flops 8598323200 | bytes 20971520 | tf_op jit(solution)/shard_map/dot_general | solution.py:57
  25.3 14.8 %fusion = f32[2048,2048]{0,1:T(8,128)} fusion(bf16[512,2048]{1,0:T(8,128)(2,1)S(1)} %fusion.37, bf16[512,2048]{1,0:T(8,128)(2,1)} %get-tuple-element.7, bf16[512,2048]{1,0:T(8,128)(2,1)} %get-tuple-element.6), kind=kOutput, calls=%fused_computation.4 | convolution fusion | flops 8606711808 | bytes 23068672 | tf_op jit(solution)/shard_map/dot_general | solution.py:58
  40.0 18.9 %pad_maximum_fusion = f32[2048,4096]{0,1:T(8,128)} fusion(f32[2048,2048]{0,1:T(8,128)} %fusion, f32[2048,2048]{0,1:T(8,128)S(1)} %fusion.4), kind=kLoop, calls=%fused_computation.2 | loop fusion | flops 8388608 | bytes 67108864 | tf_op jit(solution)/shard_map/concatenate | solution.py:60
  58.9 0.0 reduce-scatter.3.cloned.1.call-update
  58.9 0.0 reduce-scatter.5.cloned.1.call-start
  59.0 286.0 %reduce-scatter.3.cloned.1.call-done = f32[512,4096]{0,1:T(8,128)} async-done(((f32[2048,4096]{0,1:T(8,128)}), f32[512,4096]{0,1:T(8,128)}) %reduce-scatter.3.cloned.1.call-update) | async-done | bytes 8388624 | tf_op jit(solution)/shard_map/reduce_scatter | solution.py:59
  345.0 0.0 reduce-scatter.5.cloned.1.call-update
  345.0 80.6 %reduce-scatter.5.cloned.1.call-done = f32[128,4096]{0,1:T(8,128)} async-done(((f32[512,4096]{0,1:T(8,128)}), f32[128,4096]{0,1:T(8,128)}) %reduce-scatter.5.cloned.1.call-update) | async-done | bytes 2097168 | tf_op jit(solution)/shard_map/reduce_scatter | solution.py:62
  425.6 2.9 copy.8
  428.5 0.0 copy-start.3
  428.5 4.2 all-to-all-start
  432.7 0.0 copy-done.3
  432.7 0.1 bitcast_or_fusion
  432.8 0.1 reshape.48
  432.9 30.2 %all-to-all-done = f32[8,16,4096]{2,1,0:T(8,128)S(1)} async-done(((f32[8,16,4096]{2,1,0:T(8,128)}), f32[8,16,4096]{2,1,0:T(8,128)S(1)}, u32[]{:S(2)}, u32[]{:S(2)}) %all-to-all-start) | async-done | bytes 2097184 | tf_op jit(solution)/shard_map/all_to_all | solution.py:22
  463.1 0.1 reduce_sum.27
  463.3 0.0 copy-start
  463.3 0.0 copy-start.1
  463.3 24.6 %gather_fusion.1 = f32[3200]{0:T(1024)S(1)} fusion(f32[16,2048]{1,0:T(8,128)S(1)} %get-tuple-element.8, s32[3200]{0:T(1024)S(1)} %reshape.48), kind=kCustom, calls=%fused_computation.1.clone | custom fusion | bytes 51200 | tf_op jit(solution)/shard_map/jit(take_along_axis)/gather | solution.py:72
  487.9 0.0 copy-done
  487.9 0.1 reshape.56
  488.0 0.0 copy-done.1
  488.0 0.0 copy-start.4
  488.0 0.0 copy-start.5
  488.0 24.6 %gather_fusion = f32[3200]{0:T(1024)S(1)} fusion(f32[16,2048]{1,0:T(8,128)S(1)} %get-tuple-element.9, s32[3200]{0:T(1024)S(1)} %reshape.48), kind=kCustom, calls=%fused_computation.clone | custom fusion | bytes 51200 | tf_op jit(solution)/shard_map/jit(take_along_axis)/gather | solution.py:71
  512.6 0.1 reshape.51
  512.7 0.0 copy-done.4
  512.7 0.1 fusion.30
  512.8 0.0 copy-done.5
  512.9 8.4 %psum.35 = f32[2,200]{1,0:T(2,128)S(1)} all-reduce(f32[2,200]{1,0:T(2,128)S(1)} %pad_maximum_fusion.4), channel_id=1, replica_groups=mesh['gx'=4,'gy_0'=2,'gy_1'=2,'gz_0'=4,'gz_1'=2] {'gx'}, use_global_device_ids=true, to_apply=%region_5.7 | all-reduce | flops 400 | bytes 3200 | tf_op jit(solution)/shard_map/psum | solution.py:27
  521.3 5.3 psum.36
  526.6 6.9 %psum.37 = f32[2,200]{1,0:T(2,128)S(1)} all-reduce(f32[2,200]{1,0:T(2,128)S(1)} %psum.36), channel_id=1, replica_groups=mesh['gx'=4,'gy_0'=2,'gy_1'=2,'gz_0'=4,'gz_1'=2] {'gy_1'}, use_global_device_ids=true, to_apply=%region_7.9 | all-reduce | flops 400 | bytes 3200 | tf_op jit(solution)/shard_map/psum | solution.py:27
  533.5 6.1 %psum.38 = f32[2,200]{1,0:T(2,128)S(1)} all-reduce(f32[2,200]{1,0:T(2,128)S(1)} %psum.37), channel_id=1, replica_groups=mesh['gx'=4,'gy_0'=2,'gy_1'=2,'gz_0'=4,'gz_1'=2] {'gz_0'}, use_global_device_ids=true, to_apply=%region_8.10 | all-reduce | flops 400 | bytes 3200 | tf_op jit(solution)/shard_map/psum | solution.py:27
  539.5 4.3 psum.39
  (5 shorter events, 0.1 us)
Async XLA Ops:
  7.2 337.8 %reduce-scatter.3.cloned.1.call-start = ((), (), s32[]{:S(2)}) async-start(), calls=%async_computation.3 | async-start | bytes 41943040 | tf_op jit(solution)/shard_map/reduce_scatter | solution.py:59
  7.2 2.8 copy-start.2
  58.9 366.7 %reduce-scatter.5.cloned.1.call-start = ((), (), s32[]{:S(2)}) async-start(), calls=%async_computation.4 | async-start | bytes 10485760 | tf_op jit(solution)/shard_map/reduce_scatter | solution.py:62
  428.5 4.2 copy-start.3
  428.5 34.6 %all-to-all-start = ((f32[8,16,4096]{2,1,0:T(8,128)}), f32[8,16,4096]{2,1,0:T(8,128)S(1)}, u32[]{:S(2)}, u32[]{:S(2)}) async-start(f32[8,16,4096]{2,1,0:T(8,128)} %bitcast.14), calls=%async_computation.2 | async-start | bytes 4194304 | tf_op jit(solution)/shard_map/all_to_all | solution.py:22
  463.3 24.6 %copy-start = (f32[16,2048]{1,0:T(8,128)}, f32[16,2048]{1,0:T(8,128)S(1)}, u32[]{:S(2)}) copy-start(f32[16,2048]{1,0:T(8,128)S(1)} %get-tuple-element.8) | copy-start | bytes 393220
  463.3 24.7 %copy-start.1 = (f32[16,2048]{1,0:T(8,128)}, f32[16,2048]{1,0:T(8,128)S(1)}, u32[]{:S(2)}) copy-start(f32[16,2048]{1,0:T(8,128)S(1)} %get-tuple-element.9) | copy-start | bytes 393220
  488.0 24.7 %copy-start.4 = (s32[200]{0:T(256)S(1)}, s32[200]{0:T(256)}, u32[]{:S(2)}) copy-start(s32[200]{0:T(256)} %param.8) | copy-start | bytes 2404
  488.0 24.8 %copy-start.5 = (s32[200]{0:T(256)S(1)}, s32[200]{0:T(256)}, u32[]{:S(2)}) copy-start(s32[200]{0:T(256)} %param.9) | copy-start | bytes 2404
Sparse Core Ops, SparseCore 0:
  59.1 285.8 reduce-scatter.2
  347.6 77.9 reduce-scatter.4
where the time goes:
time: 553 us; the launch traced here: 551 us
  waiting for transfers between devices  397 us (72%)
  local copies, waits for them, and re-layouts  55.7 us (10%)
  blocking collectives  31 us (6%)
  matrix products  27.5 us (5%)
  other arithmetic  21.1 us (4%)
  between operations  14.2 us (3%)
    reduce_scatter x1, waiting for transfers between devices, on_device(): lax.psum_scatter(jnp.concatenate([real_rows, imag_rows], 1), 'gx', scatte...  286 us
    reduce_scatter x1, waiting for transfers between devices, on_device(): by_gy = lax.psum_scatter(by_gx, GY, scatter_dimension=0, tiled=True)  80.6 us
    psum x5, blocking collectives, over_axes(): return functools.reduce(lax.psum, axes, array)  31 us
    all_to_all x1, waiting for transfers between devices, sent_and_summed(): lax.all_to_all(parts, axis, split_axis=0, concat_axis=0, tiled=True)  30.2 us
    gather x3, local copies, waits for them, and re-layouts, on_device(): picked_real = jnp.take_along_axis(density_real, partner, axis=1)  24.7 us
    gather x2, local copies, waits for them, and re-layouts, on_device(): picked_imag = jnp.take_along_axis(density_imag, partner, axis=1)  24.7 us
    concatenate x1, other arithmetic, on_device(): jnp.concatenate([real_rows, imag_rows], 1)  18.9 us
    dot_general x1, matrix products, on_device(): lax.dot_general(crossed, stacked, dims, preferred_element_type=jnp.float32)  14.8 us
  transfers between devices with their start and end apart: 3, of which 3 were waited for; matrix products, arithmetic and copies ran while one was open for 0% of the time, Pallas kernels for 0%

commit v1 on v0

v1 whole, which is shorter than its diff:
```python
import functools

import jax
import jax.numpy as jnp
from jax import lax
from jax.experimental import pallas as pl
from jax.experimental.pallas import tpu as pltpu
from jax.sharding import Mesh
from jax.sharding import PartitionSpec as P

ORDER = 2048
COLS = 65536
DEPTH = 512
TERMS = 200
TERMS_PAD = 256
AXES = ("gx", "gy_0", "gy_1", "gz_0", "gz_1")
ROWS = (slice(0, 88), slice(88, 176), slice(176, 256))
ROW_HALVES = (
    (slice(0, 48), slice(48, 88)),
    (slice(88, 136), slice(136, 176)),
    (slice(176, 216), slice(216, 256)),
)
FAR, PURE, ACC = 0, 1, 2
LAG = 4
LO, HI = slice(0, 2), slice(2, 4)
HALF = (LO, HI)


def offset(r):
    return lax.rem(2 + r + r // 2 + 2 * (r // 3), 4)


def remote(src, dst, send, recv, device):
    return pltpu.make_async_remote_copy(
        src_ref=src,
        dst_ref=dst,
        send_sem=send,
        recv_sem=recv,
        device_id=device,
        device_id_type=pl.DeviceIdType.MESH,
    )


def parity(values):
    values = values ^ (values >> 8)
    values = values ^ (values >> 4)
    values = values ^ (values >> 2)
    values = values ^ (values >> 1)
    return values & 1


def kernel(
    amp, px, pz, pph,
    out_re, out_im, out_ex,
    s, t, p, stage, cross, ph1, ph2, ph3, flipped, direct, mirror, part,
    in_sem, core_ss, core_rs, ss1, rs1, ss2, rs2, ss3, rs3,
    dss, drs, mss, mrs, ess, ers,
):
    x0 = lax.axis_index("gx")
    zh = lax.axis_index("gy_0")
    core = lax.axis_index("gy_1")
    y0 = lax.axis_index("gz_0")
    zl = lax.axis_index("gz_1")
    z0 = 2 * zh + zl
    me = x0 * 32 + zh * 16 + core * 8 + y0 * 2 + zl

    def at_x(step):
        return {"gx": lax.rem(x0 + step, 4)}

    def at_y(step):
        return {"gz_0": lax.rem(y0 + step, 4)}

    def at_z(step):
        z = lax.rem(z0 + step, 4)
        return {"gy_0": z // 2, "gz_1": lax.rem(z, 2)}

    along = (at_x, at_y, at_z)
    other_core = {"gy_1": 1 - core}

    load = pltpu.make_async_copy(amp, s, in_sem)
    load.start()
    barrier = pltpu.get_barrier_semaphore()
    partners = [other_core] + [f(k) for f in along for k in (1, 3)]
    for device in partners:
        pl.semaphore_signal(barrier, inc=1, device_id=device, device_id_type=pl.DeviceIdType.MESH)
    pl.semaphore_wait(barrier, len(partners))
    load.wait()

    def transposed(slot, block):
        first = pl.multiple_of(block * 256, 256)
        re_t = s[0, :, pl.ds(first, 256)].T
        im_t = s[1, :, pl.ds(first, 256)].T
        t[slot, 0] = re_t
        t[slot, 1] = im_t
        t[slot, 2] = -re_t

    def block_product(slot, block, y, x, half, dst):
        col = 2 * x + half
        first = pl.multiple_of(col * 256, 256)

        def product(k):
            return jnp.dot(
                t[slot, k], s[0, :, pl.ds(first, 256)], preferred_element_type=jnp.float32
            ) + jnp.dot(
                t[slot, k + 1], s[1, :, pl.ds(first, 256)], preferred_element_type=jnp.float32
            )

        def put(value):
            dst[y, x, 2 * half] = value[:, :128]
            dst[y, x, 2 * half + 1] = value[:, 128:]

        @pl.when(block != col)
        def _():
            put(product((block - col + 8) // 8))

        @pl.when(block == col)
        def _():
            row = lax.broadcasted_iota(jnp.int32, (256, 256), 0)
            lane = lax.broadcasted_iota(jnp.int32, (256, 256), 1)
            put(jnp.where(lane >= row, product(0), product(1)))

    def unit_of(v):
        off_y, off_x = offset(v // 4), offset(lax.rem(v, 4))
        return off_y, off_x, lax.rem(y0 + off_y, 4), lax.rem(x0 + off_x, 4)

    def core_copy(v, y, x):
        return remote(stage.at[y, x], cross.at[y, x], core_ss.at[v], core_rs.at[v], other_core)

    def send1(kind, o, src, key, index, step):
        remote(
            src,
            ph1.at[(kind,) + key + (ROWS[o],)],
            ss1.at[kind, o, index],
            rs1.at[kind, o, index],
            along[o](step),
        ).start()

    def wait1(kind, o, key, index):
        ref = ph1.at[(kind,) + key + (ROWS[o],)]
        remote(ref, ref, ss1.at[kind, o, index], rs1.at[kind, o, index], along[o](1)).wait_recv()

    def finish(v):
        off_y, off_x, y, x = unit_of(v)
        core_copy(v, y, x).wait_recv()
        for z in range(4):
            p[y, x, z] += cross[y, x, z]
        for o, off, line in ((0, off_x, y), (1, off_y, x)):
            @pl.when(off == 2)
            def _(o=o, line=line):
                for h, step in ((0, 1), (1, 3)):
                    send1(FAR, o, p.at[y, x, HALF[h], ROWS[o]], (line, HALF[h]), 2 * line + h, step)

            @pl.when(off == 1)
            def _(o=o, line=line):
                send1(PURE, o, p.at[y, x, HI, ROWS[o]], (line, HI), 2 * line + 1, 1)

            @pl.when(off == 3)
            def _(o=o, line=line):
                send1(PURE, o, p.at[y, x, LO, ROWS[o]], (line, LO), 2 * line, 3)

        up = lax.rem(v, 2)
        far, right, left = (lax.rem(z0 + k, 4) for k in (2, 1, 3))

        @pl.when(up == 0)
        def _():
            send1(FAR, 2, p.at[y, x, far, ROWS[2]], (y, x), 4 * y + x, 1)
            send1(PURE, 2, p.at[y, x, left, ROWS[2]], (y, x), 4 * y + x, 3)

        @pl.when(up == 1)
        def _():
            send1(FAR, 2, p.at[y, x, far, ROWS[2]], (y, x), 4 * y + x, 3)
            send1(PURE, 2, p.at[y, x, right, ROWS[2]], (y, x), 4 * y + x, 1)

    def forward(v):
        off_y, off_x, y, x = unit_of(v)
        for o, off, line in ((0, off_x, y), (1, off_y, x)):
            for h, step in ((0, 1), (1, 3)):
                @pl.when(off == step)
                def _(o=o, line=line, h=h, step=step):
                    key, index = (line, HALF[h]), 2 * line + h
                    wait1(FAR, o, key, index)
                    p[y, x, HALF[h], ROWS[o]] += ph1[FAR, line, HALF[h], ROWS[o]]
                    send1(ACC, o, p.at[y, x, HALF[h], ROWS[o]], key, index, step)

        wait1(FAR, 2, (y, x), 4 * y + x)
        for h, step in ((0, 1), (1, 3)):
            @pl.when(lax.rem(v, 2) == h)
            def _(step=step):
                z = lax.rem(z0 + step, 4)
                p[y, x, z, ROWS[2]] += ph1[FAR, y, x, ROWS[2]]
                send1(ACC, 2, p.at[y, x, z, ROWS[2]], (y, x), 4 * y + x, step)

    def step(u, carry):
        _, _, y, x = unit_of(u)

        @pl.when(lax.rem(u, 4) == 0)
        def _():
            transposed(0, 4 * (1 - core) + y)
            transposed(1, 4 * core + y)

        for half in range(2):
            block_product(0, 4 * (1 - core) + y, y, x, half, stage)
        core_copy(u, y, x).start()
        for half in range(2):
            block_product(1, 4 * core + y, y, x, half, p)

        @pl.when(u >= 1)
        def _():
            finish(u - 1)

        @pl.when(u >= 1 + LAG)
        def _():
            forward(u - 1 - LAG)

        return carry

    lax.fori_loop(0, 16, step, 0)
    finish(15)
    lax.fori_loop(15 - LAG, 16, lambda v, carry: (forward(v), carry)[1], 0)

    def held(o, b, cs):
        if o == 0:
            return (b, x0, cs, ROWS[0])
        if o == 1:
            return (y0, cs, b, ROWS[1])
        return (cs, b, z0, ROWS[2])

    def landed(o, b, cs):
        return (b, cs, ROWS[0]) if o == 0 else (cs, b, ROWS[o])

    origin2 = (y0, z0, x0)
    origin3 = (z0, x0, y0)
    along2 = (at_y, at_z, at_x)
    along3 = (at_z, at_x, at_y)
    every = slice(0, 4)

    def take1(o, b, first):
        if o == 0:
            for kind in (PURE, ACC):
                for h in range(2):
                    wait1(kind, 0, (b, HALF[h]), 2 * b + h)
        elif o == 1:
            if first:
                for kind in (PURE, ACC):
                    for line in range(4):
                        for h in range(2):
                            wait1(kind, 1, (line, HALF[h]), 2 * line + h)
        else:
            for kind in (PURE, ACC):
                for y in range(4):
                    wait1(kind, 2, (y, b), 4 * y + b)
        for c in range(4):
            p[held(o, b, c)] += ph1[(PURE,) + landed(o, b, c)] + ph1[(ACC,) + landed(o, b, c)]

    def copy2(kind, o, src, h, step):
        return remote(
            src, ph2.at[kind, HALF[h], ROWS[o]], ss2.at[kind, o, h], rs2.at[kind, o, h],
            along2[o](step),
        )

    def wait2(kind, o, h):
        copy2(kind, o, ph2.at[kind, HALF[h], ROWS[o]], h, 1).wait_recv()

    def at2(o, k):
        return lax.rem(origin2[o] + k, 4)

    for o in range(3):
        b = at2(o, 2)
        take1(o, b, True)
        for h, step in ((0, 1), (1, 3)):
            copy2(FAR, o, p.at[held(o, b, HALF[h])], h, step).start()
    for o in range(3):
        for h, step in ((1, 1), (0, 3)):
            b = at2(o, step)
            take1(o, b, False)
            copy2(PURE, o, p.at[held(o, b, HALF[h])], h, step).start()
    for o in range(3):
        for h, step in ((0, 1), (1, 3)):
            b = at2(o, step)
            wait2(FAR, o, h)
            p[held(o, b, HALF[h])] += ph2[FAR, HALF[h], ROWS[o]]
            copy2(ACC, o, p.at[held(o, b, HALF[h])], h, step).start()
    for o in range(3):
        take1(o, origin2[o], False)

    def own(o, c, rows):
        return held(o, origin2[o], c)[:3] + (rows,)

    def copy3(kind, o, src, h, step):
        return remote(
            src, ph3.at[kind, ROW_HALVES[o][h]], ss3.at[kind, o, h], rs3.at[kind, o, h],
            along3[o](step),
        )

    def wait3(kind, o, h):
        copy3(kind, o, ph3.at[kind, ROW_HALVES[o][h]], h, 1).wait_recv()

    def take2(o, c):
        p[own(o, c, ROWS[o])] += ph2[PURE, c, ROWS[o]] + ph2[ACC, c, ROWS[o]]

    def at3(o, k):
        return lax.rem(origin3[o] + k, 4)

    for o in range(3):
        for kind in (PURE, ACC):
            for h in range(2):
                wait2(kind, o, h)
        c = at3(o, 2)
        take2(o, c)
        for h, step in ((0, 1), (1, 3)):
            copy3(FAR, o, p.at[own(o, c, ROW_HALVES[o][h])], h, step).start()
    for o in range(3):
        for h, step in ((1, 1), (0, 3)):
            c = at3(o, step)
            take2(o, c)
            copy3(PURE, o, p.at[own(o, c, ROW_HALVES[o][h])], h, step).start()
    for o in range(3):
        for h, step in ((0, 1), (1, 3)):
            c = at3(o, step)
            wait3(FAR, o, h)
            p[own(o, c, ROW_HALVES[o][h])] += ph3[FAR, ROW_HALVES[o][h]]
            copy3(ACC, o, p.at[own(o, c, ROW_HALVES[o][h])], h, step).start()
    for o in range(3):
        take2(o, origin3[o])
    for o in range(3):
        for kind in (PURE, ACC):
            for h in range(2):
                wait3(kind, o, h)
    block = p[y0, x0, z0] + ph3[PURE] + ph3[ACC]
    p[y0, x0, z0] = block
    flipped[...] = block.T

    row_block = 4 * core + y0
    col_block = 4 * x0 + z0

    def device(e):
        return {
            "gx": e // 32,
            "gy_0": lax.rem(e // 16, 2),
            "gy_1": lax.rem(e // 8, 2),
            "gz_0": lax.rem(e // 2, 4),
            "gz_1": lax.rem(e, 2),
        }

    def direct_copy(k):
        e = 16 * row_block + k
        return e, remote(
            p.at[y0, x0, z0, pl.ds(16 * k, 16)], direct.at[col_block],
            dss.at[k], drs.at[col_block], device(e),
        )

    def mirror_copy(k):
        e = 8 * col_block + k
        return e, remote(
            flipped.at[pl.ds(16 * k, 16)], mirror.at[row_block],
            mss.at[k], mrs.at[row_block], device(e),
        )

    for k in range(16):
        e, copy = direct_copy(k)

        @pl.when(e != me)
        def _(copy=copy):
            copy.start()

        @pl.when(e == me)
        def _(k=k):
            direct[col_block] = p[y0, x0, z0, pl.ds(16 * k, 16)]

    for k in range(8):
        e, copy = mirror_copy(k)

        @pl.when(e != me)
        def _(copy=copy):
            copy.start()

        @pl.when(e == me)
        def _(k=k):
            mirror[row_block] = flipped[pl.ds(16 * k, 16)]

    row = lax.broadcasted_iota(jnp.int32, (256, 128), 0)
    lane = lax.broadcasted_iota(jnp.int32, (256, 128), 1)
    moved = block
    for bit in range(7):
        hop = 1 << bit
        swapped = jnp.where(
            (lane & hop) != 0, pltpu.roll(moved, hop, 1), pltpu.roll(moved, 128 - hop, 1)
        )
        moved = jnp.where((row & hop) != 0, swapped, moved)
    in_row = 256 * row_block + row
    in_col = 128 * col_block + ((row & 127) ^ lane)
    upper = jnp.where(in_col >= in_row, moved, 0.0)
    lower = jnp.where(in_col >= in_row, 0.0, moved)
    xs, zs, phase = px[...], pz[...], pph[...]
    pick_row = lax.broadcasted_iota(jnp.int32, (128, TERMS), 0)
    pick = jnp.where(pick_row == (xs & 127), 1.0, 0.0).astype(jnp.float32)
    dot = functools.partial(
        jnp.dot, preferred_element_type=jnp.float32, precision=lax.Precision.HIGHEST
    )
    term_row = 256 * row_block + lax.broadcasted_iota(jnp.int32, (256, TERMS), 0)
    sign = (1 - 2 * parity(term_row & zs)).astype(jnp.float32)
    sign = jnp.where(((term_row >> 7) ^ (xs >> 7)) == col_block, sign, 0.0)
    even = (1 - parity(xs & zs)).astype(jnp.float32)
    real_weight = jnp.where(xs == 0, 1.0, 2.0 * even)
    imag_weight = 2.0 - 2.0 * even
    sum_re = real_weight * jnp.sum(sign * dot(upper, pick), axis=0, keepdims=True)
    sum_im = imag_weight * jnp.sum(sign * dot(lower, pick), axis=0, keepdims=True)
    phase_re = jnp.where(phase == 0, 1.0, jnp.where(phase == 2, -1.0, 0.0))
    phase_im = jnp.where(phase == 1, 1.0, jnp.where(phase == 3, -1.0, 0.0))
    scale = 1.0 / COLS
    here = jnp.concatenate(
        [
            (phase_re * sum_re - phase_im * sum_im) * scale,
            (phase_re * sum_im + phase_im * sum_re) * scale,
            jnp.zeros((6, TERMS), jnp.float32),
        ],
        axis=0,
    )

    for stage_no, (mine, count, where) in enumerate(
        ((core, 2, lambda k: other_core), (x0, 4, at_x), (y0, 4, at_y), (z0, 4, at_z))
    ):
        part[stage_no, mine, :, :TERMS] = here
        for k in range(1, count):
            remote(
                part.at[stage_no, mine], part.at[stage_no, mine],
                ess.at[stage_no, k], ers.at[stage_no, mine], where(k),
            ).start()
        for k in range(1, count):
            source = lax.rem(mine + k, count)
            slot = part.at[stage_no, source]
            remote(
                slot, slot, ess.at[stage_no, k], ers.at[stage_no, source], where(k)
            ).wait_recv()
        here = part[stage_no, 0, :, :TERMS]
        for k in range(1, count):
            here = here + part[stage_no, k, :, :TERMS]
    out_ex[...] = here[:2]

    for k in range(16):
        sender_x, sender_z = k // 4, k % 4
        sender = (sender_x * 32 + (sender_z // 2) * 16 + (me // 64) * 8
                  + lax.rem(me // 16, 4) * 2 + sender_z % 2)

        @pl.when(sender != me)
        def _(k=k):
            ref = direct.at[k]
            remote(ref, ref, dss.at[0], drs.at[k], other_core).wait_recv()

    for k in range(8):
        sender_core, sender_y = k // 4, k % 4
        sender_x, sender_z = me // 32, lax.rem(me // 8, 4)
        sender = (sender_x * 32 + (sender_z // 2) * 16 + sender_core * 8
                  + sender_y * 2 + lax.rem(sender_z, 2))

        @pl.when(sender != me)
        def _(k=k):
            ref = mirror.at[k]
            remote(ref, ref, mss.at[0], mrs.at[k], other_core).wait_recv()

    row = 16 * me + lax.broadcasted_iota(jnp.int32, (16, 128), 0)
    lane = lax.broadcasted_iota(jnp.int32, (16, 128), 1)
    for k in range(16):
        given = direct[k] * scale
        turned = mirror[k // 2, :, 128 * (k % 2) : 128 * (k % 2) + 128] * scale
        col = 128 * k + lane
        out_re[:, 128 * k : 128 * k + 128] = jnp.where(col >= row, given, turned)
        out_im[:, 128 * k : 128 * k + 128] = jnp.where(
            col < row, given, jnp.where(col == row, 0.0, -turned)
        )

    def sent_unit(v, carry):
        _, _, y, x = unit_of(v)
        core_copy(v, y, x).wait_send()
        for kind in range(3):
            ref = ph1.at[kind, 0, 0, ROWS[2]]
            remote(ref, ref, ss1.at[kind, 2, v], rs1.at[kind, 2, v], at_z(1)).wait_send()
        return carry

    lax.fori_loop(0, 16, sent_unit, 0)

    def sent_pair(v, carry):
        for kind in range(3):
            for o in range(2):
                ref = ph1.at[kind, 0, LO, ROWS[o]]
                remote(ref, ref, ss1.at[kind, o, v], rs1.at[kind, o, v], at_x(1)).wait_send()
        return carry

    lax.fori_loop(0, 8, sent_pair, 0)
    for kind in range(3):
        for o in range(3):
            for h in range(2):
                copy2(kind, o, ph2.at[kind, HALF[h], ROWS[o]], h, 1).wait_send()
                copy3(kind, o, ph3.at[kind, ROW_HALVES[o][h]], h, 1).wait_send()
    for k in range(16):
        e, copy = direct_copy(k)

        @pl.when(e != me)
        def _(copy=copy):
            copy.wait_send()

    for k in range(8):
        e, copy = mirror_copy(k)

        @pl.when(e != me)
        def _(copy=copy):
            copy.wait_send()

    for stage_no, count in enumerate((2, 4, 4, 4)):
        for k in range(1, count):
            slot = part.at[stage_no, 0]
            remote(
                slot, slot, ess.at[stage_no, k], ers.at[stage_no, 0], other_core
            ).wait_send()


def on_device(amplitudes, pauli_x, pauli_z, pauli_phase):
    vmem = pl.BlockSpec(memory_space=pltpu.VMEM)
    f32 = jnp.float32
    dma = pltpu.SemaphoreType.DMA
    return pl.pallas_call(
        kernel,
        out_shape=(
            jax.ShapeDtypeStruct((16, ORDER), f32),
            jax.ShapeDtypeStruct((16, ORDER), f32),
            jax.ShapeDtypeStruct((2, TERMS), f32),
        ),
        in_specs=[pl.BlockSpec(memory_space=pl.ANY), vmem, vmem, vmem],
        out_specs=(vmem, vmem, vmem),
        scratch_shapes=[
            pltpu.VMEM((2, DEPTH, ORDER), jnp.bfloat16),
            pltpu.VMEM((2, 3, 256, DEPTH), jnp.bfloat16),
            pltpu.VMEM((4, 4, 4, 256, 128), f32),
            pltpu.VMEM((4, 4, 4, 256, 128), f32),
            pltpu.VMEM((4, 4, 4, 256, 128), f32),
            pltpu.VMEM((3, 4, 4, 256, 128), f32),
            pltpu.VMEM((3, 4, 256, 128), f32),
            pltpu.VMEM((3, 256, 128), f32),
            pltpu.VMEM((128, 256), f32),
            pltpu.VMEM((16, 16, 128), f32),
            pltpu.VMEM((8, 16, 256), f32),
            pltpu.VMEM((4, 4, 8, TERMS_PAD), f32),
            dma(()),
            dma((16,)),
            dma((16,)),
            dma((3, 3, 16)),
            dma((3, 3, 16)),
            dma((3, 3, 2)),
            dma((3, 3, 2)),
            dma((3, 3, 2)),
            dma((3, 3, 2)),
            dma((16,)),
            dma((16,)),
            dma((8,)),
            dma((8,)),
            dma((4, 4)),
            dma((4, 4)),
        ],
        compiler_params=pltpu.CompilerParams(
            collective_id=0, has_side_effects=True, vmem_limit_bytes=60 * 1024 * 1024
        ),
    )(amplitudes, pauli_x.reshape(1, TERMS), pauli_z.reshape(1, TERMS), pauli_phase.reshape(1, TERMS))


def solution(mesh):
    finer = Mesh(mesh.devices.reshape(mesh.shape["gx"], 2, 2, 4, 2), AXES)
    return jax.shard_map(
        on_device,
        mesh=finer,
        in_specs=(P(None, AXES, None), P(), P(), P()),
        out_specs=(P(AXES, None), P(AXES, None), P()),
        check_vma=False,
    )
```

time: 553 us -> 83.3 us (0.15)
  waiting for transfers between devices: 397 us -> 0 us
  Pallas kernels: 0 us -> 78.1 us
  local copies, waits for them, and re-layouts: 55.7 us -> 4.38 us
  blocking collectives: 31 us -> 0 us
  matrix products: 27.5 us -> 0 us
  other arithmetic: 21.1 us -> 0 us
  between operations: 14.2 us -> 0.64 us
    reduce_scatter x2 -> x0, waiting for transfers between devices: 367 us -> none  [the longest x1 286 us: on_device(): lax.psum_scatter(jnp.concatenate([real_rows, imag_rows], 1), 'gx', scatte...]
    pallas_call x0 -> x1, Pallas kernels: none -> 78.1 us  [on_device(): pl.pallas_call(kernel, out_shape=(jax.ShapeDtypeStruct((16, ORDER), f32),...]
    gather x5 -> x0, local copies, waits for them, and re-layouts: 49.4 us -> none  [the longest x3 24.7 us: on_device(): picked_real = jnp.take_along_axis(density_real, partner, axis=1)]
    psum x5 -> x0, blocking collectives: 31 us -> none  [over_axes(): return functools.reduce(lax.psum, axes, array)]
    all_to_all x1 -> x0, waiting for transfers between devices: 30.2 us -> none  [sent_and_summed(): lax.all_to_all(parts, axis, split_axis=0, concat_axis=0, tiled=True)]
    dot_general x2 -> x0, matrix products: 27.5 us -> none  [the longest x1 14.8 us: on_device(): lax.dot_general(crossed, stacked, dims, preferred_element_type=jnp.float32)]
    concatenate x1 -> x0, other arithmetic: 18.9 us -> none  [on_device(): jnp.concatenate([real_rows, imag_rows], 1)]
  transfers between devices with their start and end apart: 3 -> 0, of which waited for: 3 -> 0; matrix products, arithmetic and copies ran while one was open for 0% -> 0% of each run, Pallas kernels for 0% -> 0%
where the time goes in v1:
time: 83.3 us; the launch traced here: 83.2 us
  Pallas kernels  78.1 us (94%)
  local copies, waits for them, and re-layouts  4.38 us (5%)
    pallas_call x1, Pallas kernels, on_device(): pl.pallas_call(kernel, out_shape=(jax.ShapeDtypeStruct((16, ORDER), f32),...  78.1 us
    unnamed x3, local copies, waits for them, and re-layouts  4.38 us

profile of v1, /device:TPU:1, one launch (start us, length us, event | category | flops | bytes accessed | tf_op | source)
XLA Modules:
  0.0 83.2 jit_solution(6169098182982154541)
XLA Ops:
  0.6 78.1 %shard_map.67 = (f32[16,2048]{1,0:T(8,128)}, f32[16,2048]{1,0:T(8,128)}, f32[2,200]{1,0:T(2,128)}) custom-call(bf16[2,512,2048]{2,1,0:T(8,128)(2,1)} %amp.1, s32[1,200]{1,0:T(1,128)} %bitcast.3, s32[1,200]{1,0:T(1,128)} %bitcast.4, s32[1,200]{1,0:T(1,128)} %bitcast.5), custom_call_target="tpu_custom_call" | custom-call | tf_op jit(solution)/shard_map/pallas_call | solution.py:521
  78.8 1.6 %copy.10 = f32[16,2048]{1,0:T(8,128)} copy(f32[16,2048]{1,0:T(8,128)} %get-tuple-element.6) | data formatting | bytes 262144
  80.3 1.6 %copy.11 = f32[16,2048]{1,0:T(8,128)} copy(f32[16,2048]{1,0:T(8,128)} %get-tuple-element.7) | data formatting | bytes 262144
  81.9 1.2 %copy.12 = f32[2,200]{1,0:T(2,128)} copy(f32[2,200]{1,0:T(2,128)} %get-tuple-element.8) | data formatting | bytes 3200

commit v2 on v0

v2 whole, which is shorter than its diff:
```python
import functools

import jax
import jax.numpy as jnp
from jax import lax
from jax.experimental import pallas as pl
from jax.experimental.pallas import tpu as pltpu
from jax.sharding import Mesh
from jax.sharding import PartitionSpec as P

ORDER = 2048
COLS = 65536
DEPTH = 512
TERMS = 200
TERMS_PAD = 256
AXES = ("gx", "gy_0", "gy_1", "gz_0", "gz_1")
ROWS = (slice(0, 88), slice(88, 176), slice(176, 256))
FAR, PURE, ACC = 0, 1, 2
LAG = 3
BASE = (0, 8, 16)
LO, HI = slice(0, 2), slice(2, 4)
HALF = (LO, HI)


def offset(r):
    return lax.rem(2 + r + r // 2 + 2 * (r // 3), 4)


def remote(src, dst, send, recv, device):
    return pltpu.make_async_remote_copy(
        src_ref=src,
        dst_ref=dst,
        send_sem=send,
        recv_sem=recv,
        device_id=device,
        device_id_type=pl.DeviceIdType.MESH,
    )


def parity(values):
    values = values ^ (values >> 8)
    values = values ^ (values >> 4)
    values = values ^ (values >> 2)
    values = values ^ (values >> 1)
    return values & 1


def kernel(
    amp, px, pz, pph,
    out_re, out_im, out_ex,
    s, t, p, stage, cross, ph1, ph2, ph3, flipped, direct, mirror, weights, part0, part1,
    in_sem, core_ss, core_rs, ss1, rs1, ss2, rs2, ss3, rs3,
    dss, drs, mss, mrs, ess, ers,
):
    x0 = lax.axis_index("gx")
    zh = lax.axis_index("gy_0")
    core = lax.axis_index("gy_1")
    y0 = lax.axis_index("gz_0")
    zl = lax.axis_index("gz_1")
    z0 = 2 * zh + zl
    me = x0 * 32 + zh * 16 + core * 8 + y0 * 2 + zl

    def at_x(step):
        return {"gx": lax.rem(x0 + step, 4)}

    def at_y(step):
        return {"gz_0": lax.rem(y0 + step, 4)}

    def at_z(step):
        z = lax.rem(z0 + step, 4)
        return {"gy_0": z // 2, "gz_1": lax.rem(z, 2)}

    along = (at_x, at_y, at_z)
    along2 = (at_y, at_z, at_x)
    along3 = (at_z, at_x, at_y)
    origin2 = (y0, z0, x0)
    origin3 = (z0, x0, y0)
    other_core = {"gy_1": 1 - core}
    blocks = (4 * (1 - core), 4 * core)

    def transposed(slot, y):
        first = pl.multiple_of((blocks[slot] + y) * 256, 256)
        re_t = s[:DEPTH, pl.ds(first, 256)].T
        im_t = s[DEPTH:, pl.ds(first, 256)].T
        t[slot, :, :DEPTH] = re_t
        t[slot, :, DEPTH : 2 * DEPTH] = im_t
        t[slot, :, 2 * DEPTH :] = -re_t

    def factor(slot, imag):
        return t[slot, :, pl.ds(pl.multiple_of(imag * DEPTH, DEPTH), 2 * DEPTH)]

    def column(col):
        return s[:, pl.ds(pl.multiple_of(col * 256, 256), 256)]

    dot = functools.partial(jnp.dot, preferred_element_type=jnp.float32)

    def products(y, x):
        for half in range(2):
            col = 2 * x + half
            left = jnp.concatenate(
                [factor(slot, (blocks[slot] + y - col + 7) // 8) for slot in range(2)], axis=0
            )
            value = dot(left, column(col))
            for slot, dst in ((0, stage), (1, p)):
                for k in range(2):
                    dst[y, x, 2 * half + k] = value[
                        256 * slot : 256 * slot + 256, 128 * k : 128 * k + 128
                    ]

    def mend(y, x):
        for slot, dst in ((0, stage), (1, p)):
            block = blocks[slot] + y

            @pl.when(block // 2 == x)
            def _(slot=slot, dst=dst, block=block):
                imag = dot(factor(slot, 1), column(block))
                row = lax.broadcasted_iota(jnp.int32, (256, 128), 0)
                lane = lax.broadcasted_iota(jnp.int32, (256, 128), 1)
                for k in range(2):
                    z = 2 * lax.rem(block, 2) + k
                    dst[y, x, z] = jnp.where(
                        lane + 128 * k >= row, dst[y, x, z], imag[:, 128 * k : 128 * k + 128]
                    )

    def unit_of(v):
        off_y, off_x = offset(v // 4), offset(lax.rem(v, 4))
        return off_y, off_x, lax.rem(y0 + off_y, 4), lax.rem(x0 + off_x, 4)

    def core_copy(v, y, x):
        return remote(stage.at[y, x], cross.at[y, x], core_ss.at[0], core_rs.at[v], other_core)

    def copy1(kind, o, src, key, index, step):
        return remote(
            src,
            ph1.at[(kind,) + key + (ROWS[o],)],
            ss1.at[kind, o],
            rs1.at[kind, BASE[o] + index],
            along[o](step),
        )

    def send1(kind, o, src, key, index, step):
        copy1(kind, o, src, key, index, step).start()

    def wait1(kind, o, key, index):
        copy1(kind, o, ph1.at[(kind,) + key + (ROWS[o],)], key, index, 1).wait_recv()

    def add_cross(y, x):
        for z in range(4):
            p[y, x, z] += cross[y, x, z]

    def finish(v):
        off_y, off_x, y, x = unit_of(v)
        for o, off, line in ((0, off_x, y), (1, off_y, x)):
            @pl.when(off == 2)
            def _(o=o, line=line):
                for h, step in ((0, 1), (1, 3)):
                    send1(FAR, o, p.at[y, x, HALF[h], ROWS[o]], (line, HALF[h]), 2 * line + h, step)

            @pl.when(off == 1)
            def _(o=o, line=line):
                send1(PURE, o, p.at[y, x, HI, ROWS[o]], (line, HI), 2 * line + 1, 1)

            @pl.when(off == 3)
            def _(o=o, line=line):
                send1(PURE, o, p.at[y, x, LO, ROWS[o]], (line, LO), 2 * line, 3)

        up = lax.rem(v, 2)
        far, right, left = (lax.rem(z0 + k, 4) for k in (2, 1, 3))

        @pl.when(up == 0)
        def _():
            send1(FAR, 2, p.at[y, x, far, ROWS[2]], (y, x), 4 * y + x, 1)
            send1(PURE, 2, p.at[y, x, left, ROWS[2]], (y, x), 4 * y + x, 3)

        @pl.when(up == 1)
        def _():
            send1(FAR, 2, p.at[y, x, far, ROWS[2]], (y, x), 4 * y + x, 3)
            send1(PURE, 2, p.at[y, x, right, ROWS[2]], (y, x), 4 * y + x, 1)

    def forward(v):
        off_y, off_x, y, x = unit_of(v)
        for o, off, line in ((0, off_x, y), (1, off_y, x)):
            for h, step in ((0, 1), (1, 3)):
                @pl.when(off == step)
                def _(o=o, line=line, h=h, step=step):
                    key, index = (line, HALF[h]), 2 * line + h
                    wait1(FAR, o, key, index)
                    p[y, x, HALF[h], ROWS[o]] += ph1[FAR, line, HALF[h], ROWS[o]]
                    send1(ACC, o, p.at[y, x, HALF[h], ROWS[o]], key, index, step)

        wait1(FAR, 2, (y, x), 4 * y + x)
        for h, step in ((0, 1), (1, 3)):
            @pl.when(lax.rem(v, 2) == h)
            def _(step=step):
                z = lax.rem(z0 + step, 4)
                p[y, x, z, ROWS[2]] += ph1[FAR, y, x, ROWS[2]]
                send1(ACC, 2, p.at[y, x, z, ROWS[2]], (y, x), 4 * y + x, step)

    def held(o, b, cs):
        if o == 0:
            return (b, x0, cs, ROWS[0])
        if o == 1:
            return (y0, cs, b, ROWS[1])
        return (cs, b, z0, ROWS[2])

    def landed(o, b, cs):
        return (b, cs, ROWS[0]) if o == 0 else (cs, b, ROWS[o])

    def at2(o, k):
        return lax.rem(origin2[o] + k, 4)

    def at3(o, k):
        return lax.rem(origin3[o] + k, 4)

    groups = (
        ((LO, 0, 0), (HI, 1, 1)),
        ((LO, 0, 0), (HI, 1, 1)),
        tuple((at3(2, k), n % 2, n) for n, k in enumerate((2, 3, 1, 0))),
    )

    def take1(o, b, cs, lines=None):
        if o == 0:
            for kind in (PURE, ACC):
                for h in range(2):
                    wait1(kind, 0, (b, HALF[h]), 2 * b + h)
        elif o == 2:
            for kind in (PURE, ACC):
                wait1(kind, 2, (cs, b), 4 * cs + b)
        for c in range(4) if o < 2 else (cs,):
            p[held(o, b, c)] += ph1[(PURE,) + landed(o, b, c)] + ph1[(ACC,) + landed(o, b, c)]

    def all_of_order1():
        for kind in (PURE, ACC):
            for line in range(4):
                for h in range(2):
                    wait1(kind, 1, (line, HALF[h]), 2 * line + h)

    def copy2(kind, o, src, group, step):
        cs, _, n = group
        return remote(
            src, ph2.at[kind, cs, ROWS[o]], ss2.at[kind, o], rs2.at[kind, o, n], along2[o](step)
        )

    def wait2(kind, o, group):
        copy2(kind, o, ph2.at[kind, group[0], ROWS[o]], group, 1).wait_recv()

    def send2(kind, o, group, step):
        b = at2(o, 2 if kind == FAR else step)
        copy2(kind, o, p.at[held(o, b, group[0])], group, step).start()

    UP = (1, 3)
    DOWN = (3, 1)

    def accumulate2(o, group):
        cs, h, _ = group
        wait2(FAR, o, group)
        p[held(o, at2(o, UP[h]), cs)] += ph2[FAR, cs, ROWS[o]]
        send2(ACC, o, group, UP[h])

    def whole2(o):
        for group in groups[o]:
            send2(FAR, o, group, UP[group[1]])

    def pure2(o, step):
        for group in groups[o]:
            if DOWN[group[1]] == step:
                send2(PURE, o, group, step)

    def open2(n):
        group = groups[2][n]
        cs, h, _ = group
        take1(2, at2(2, 2), cs)
        send2(FAR, 2, group, UP[h])
        take1(2, at2(2, DOWN[h]), cs)
        send2(PURE, 2, group, DOWN[h])
        take1(2, at2(2, UP[h]), cs)

    def forwards(first, last):
        lax.fori_loop(first, last, lambda v, carry: (forward(v), carry)[1], 0)

    loads = [
        pltpu.make_async_copy(amp.at[k], s.at[pl.ds(DEPTH * k, DEPTH)], in_sem.at[k])
        for k in range(2)
    ]
    for load in loads:
        load.start()
    barrier = pltpu.get_barrier_semaphore()
    partners = [other_core] + [f(k) for f in along for k in (1, 3)]
    for device in partners:
        pl.semaphore_signal(barrier, inc=1, device_id=device, device_id_type=pl.DeviceIdType.MESH)
    for load in loads:
        load.wait()

    _, _, y, x = unit_of(0)
    for slot in range(2):
        transposed(slot, y)
    products(y, x)
    mend(y, x)
    pl.semaphore_wait(barrier, len(partners))
    core_copy(0, y, x).start()
    _, _, y, x = unit_of(1)
    products(y, x)
    mend(y, x)
    core_copy(1, y, x).start()

    def step(u, carry):
        _, _, y, x = unit_of(u)
        _, _, last_y, last_x = unit_of(u - 2)

        @pl.when(lax.rem(u, 4) == 0)
        def _():
            for slot in range(2):
                transposed(slot, y)
        core_copy(u - 2, last_y, last_x).wait_recv()
        products(y, x)
        add_cross(last_y, last_x)
        mend(y, x)
        core_copy(u, y, x).start()
        finish(u - 2)

        @pl.when(u >= 2 + LAG)
        def _():
            forward(u - 2 - LAG)

        @pl.when(u == 12)
        def _():
            take1(0, at2(0, 2), None)
            whole2(0)

        @pl.when(u == 13)
        def _():
            open2(0)

        return carry

    lax.fori_loop(2, 16, step, 0)
    def settle(v):
        _, _, y, x = unit_of(v)
        core_copy(v, y, x).wait_recv()
        add_cross(y, x)
        finish(v)

    settle(14)
    forward(11)
    take1(0, at2(0, 3), None)
    pure2(0, 3)
    accumulate2(2, groups[2][0])
    settle(15)
    forwards(12, 14)
    open2(1)
    forwards(14, 16)
    take1(0, at2(0, 1), None)
    pure2(0, 1)
    for group in groups[0]:
        accumulate2(0, group)
    all_of_order1()
    take1(1, at2(1, 2), None)
    whole2(1)
    for k in (3, 1):
        take1(1, at2(1, k), None)
        pure2(1, k)
    open2(2)
    accumulate2(2, groups[2][1])
    for group in groups[1]:
        accumulate2(1, group)
    open2(3)
    accumulate2(2, groups[2][2])
    accumulate2(2, groups[2][3])
    for o in range(2):
        take1(o, origin2[o], None)
    for c in range(4):
        take1(2, x0, c)

    def own(o, c):
        return held(o, origin2[o], c)

    def copy3(o, k, src):
        return remote(
            src, ph3.at[k - 1, ROWS[o]], ss3.at[k - 1, o], rs3.at[k - 1, o], along3[o](k)
        )

    def take2(o, c):
        p[own(o, c)] += ph2[PURE, c, ROWS[o]] + ph2[ACC, c, ROWS[o]]

    for o in (0, 2, 1):
        for group in groups[o]:
            for kind in (PURE, ACC):
                wait2(kind, o, group)
        for k in (2, 1, 3):
            c = at3(o, k)
            take2(o, c)
            copy3(o, k, p.at[own(o, c)]).start()
    for o in range(3):
        take2(o, origin3[o])

    row_block = 4 * core + y0
    col_block = 4 * x0 + z0
    xs, zs, phase = px[...], pz[...], pph[...]
    pick_row = lax.broadcasted_iota(jnp.int32, (128, TERMS), 0)
    pick = jnp.where(pick_row == (xs & 127), 1.0, 0.0).astype(jnp.bfloat16)
    term_row = 256 * row_block + lax.broadcasted_iota(jnp.int32, (256, TERMS), 0)
    sign = (1 - 2 * parity(term_row & zs)).astype(jnp.float32)
    weights[:, :TERMS] = jnp.where(((term_row >> 7) ^ (xs >> 7)) == col_block, sign, 0.0)
    even = (1 - parity(xs & zs)).astype(jnp.float32)
    scale = 1.0 / COLS
    real_weight = scale * jnp.where(xs == 0, 1.0, 2.0 * even)
    imag_weight = scale * (2.0 - 2.0 * even)
    phase_re = jnp.where(phase == 0, 1.0, jnp.where(phase == 2, -1.0, 0.0))
    phase_im = jnp.where(phase == 1, 1.0, jnp.where(phase == 3, -1.0, 0.0))

    for o in (0, 2, 1):
        for k in (1, 2, 3):
            copy3(o, k, ph3.at[k - 1, ROWS[o]]).wait_recv()
    block = p[y0, x0, z0] + ph3[0] + ph3[1] + ph3[2]
    p[y0, x0, z0] = block
    flipped[...] = block.T

    row = lax.broadcasted_iota(jnp.int32, (256, 128), 0)
    lane = lax.broadcasted_iota(jnp.int32, (256, 128), 1)
    moved = block
    for bit in range(7):
        hop = 1 << bit
        swapped = jnp.where(
            (lane & hop) != 0, pltpu.roll(moved, hop, 1), pltpu.roll(moved, 128 - hop, 1)
        )
        moved = jnp.where((row & hop) != 0, swapped, moved)
    in_row = 256 * row_block + row
    in_col = 128 * col_block + ((row & 127) ^ lane)
    high = moved.astype(jnp.bfloat16)
    rest = moved - high.astype(jnp.float32)
    middle = rest.astype(jnp.bfloat16)
    low = (rest - middle.astype(jnp.float32)).astype(jnp.bfloat16)
    upper = in_col >= in_row

    def read(keep):
        return sum(
            dot(jnp.where(keep, q.astype(jnp.float32), 0.0).astype(jnp.bfloat16), pick)
            for q in (high, middle, low)
        )

    weight = weights[:, :TERMS]
    sum_re = real_weight * jnp.sum(weight * read(upper), axis=0, keepdims=True)
    sum_im = imag_weight * jnp.sum(weight * read(~upper), axis=0, keepdims=True)
    here = jnp.concatenate(
        [phase_re * sum_re - phase_im * sum_im, phase_re * sum_im + phase_im * sum_re], axis=0
    )

    def give(here, parts, n, mine, count, where):
        parts[mine, :, :TERMS] = here
        for k in range(1, count):
            remote(
                parts.at[mine], parts.at[mine], ess.at[n], ers.at[n],
                where(lax.rem(mine + k, count)),
            ).start()

    def collect(parts, n, count):
        rest = parts.at[pl.ds(0, count - 1)]
        remote(rest, rest, ess.at[n], ers.at[n], other_core).wait_recv()
        total = parts[0, :, :TERMS]
        for k in range(1, count):
            total = total + parts[k, :, :TERMS]
        return total

    give(
        here, part0, 0, 4 * x0 + z0, 16,
        lambda k: {"gx": k // 4, "gy_0": lax.rem(k // 2, 2), "gz_1": lax.rem(k, 2)},
    )

    def device(e):
        return {
            "gx": e // 32,
            "gy_0": lax.rem(e // 16, 2),
            "gy_1": lax.rem(e // 8, 2),
            "gz_0": lax.rem(e // 2, 4),
            "gz_1": lax.rem(e, 2),
        }

    def direct_copy(k):
        e = 16 * row_block + k
        return e, remote(
            p.at[y0, x0, z0, pl.ds(16 * k, 16)], direct.at[col_block],
            dss.at[0], drs.at[0], device(e),
        )

    def mirror_copy(k):
        e = 8 * col_block + k
        return e, remote(
            flipped.at[pl.ds(16 * k, 16)], mirror.at[row_block],
            mss.at[0], mrs.at[0], device(e),
        )

    for k in range(16):
        e, copy = direct_copy(k)

        @pl.when(e != me)
        def _(copy=copy):
            copy.start()

        @pl.when(e == me)
        def _(k=k):
            direct[col_block] = p[y0, x0, z0, pl.ds(16 * k, 16)]

    for k in range(8):
        e, copy = mirror_copy(k)

        @pl.when(e != me)
        def _(copy=copy):
            copy.start()

        @pl.when(e == me)
        def _(k=k):
            mirror[row_block] = flipped[pl.ds(16 * k, 16)]

    give(
        collect(part0, 0, 16), part1, 1, 2 * y0 + core, 8,
        lambda k: {"gz_0": k // 2, "gy_1": lax.rem(k, 2)},
    )
    out_ex[...] = collect(part1, 1, 8)

    def landed_and_left(ref, ss, rs):
        copy = remote(ref, ref, ss, rs, other_core)
        copy.wait_recv()
        copy.wait_send()

    @pl.when(me // 16 == row_block)
    def _():
        landed_and_left(direct.at[pl.ds(0, 15)], dss.at[0], drs.at[0])

    @pl.when(me // 16 != row_block)
    def _():
        landed_and_left(direct, dss.at[0], drs.at[0])

    @pl.when(me // 8 == col_block)
    def _():
        landed_and_left(mirror.at[pl.ds(0, 7)], mss.at[0], mrs.at[0])

    @pl.when(me // 8 != col_block)
    def _():
        landed_and_left(mirror, mss.at[0], mrs.at[0])

    row = 16 * me + lax.broadcasted_iota(jnp.int32, (16, 128), 0)
    lane = lax.broadcasted_iota(jnp.int32, (16, 128), 1)
    for k in range(16):
        given = direct[k] * scale
        turned = mirror[k // 2, :, 128 * (k % 2) : 128 * (k % 2) + 128] * scale
        col = 128 * k + lane
        out_re[:, 128 * k : 128 * k + 128] = jnp.where(col >= row, given, turned)
        out_im[:, 128 * k : 128 * k + 128] = jnp.where(
            col < row, given, jnp.where(col == row, 0.0, -turned)
        )

    def left(ref, sem):
        remote(ref, ref, sem, core_rs.at[0], other_core).wait_send()

    left(stage, core_ss.at[0])
    for kind in range(3):
        for o in range(3):
            left(ph3.at[kind, ROWS[o]], ss3.at[kind, o])
            left(ph2.at[kind, :, ROWS[o]], ss2.at[kind, o])
            left(ph1.at[kind, :, :, ROWS[o]], ss1.at[kind, o])
    left(part0.at[pl.ds(0, 15)], ess.at[0])
    left(part1.at[pl.ds(0, 7)], ess.at[1])


def on_device(amplitudes, pauli_x, pauli_z, pauli_phase):
    vmem = pl.BlockSpec(memory_space=pltpu.VMEM)
    f32 = jnp.float32
    dma = pltpu.SemaphoreType.DMA
    return pl.pallas_call(
        kernel,
        out_shape=(
            jax.ShapeDtypeStruct((16, ORDER), f32),
            jax.ShapeDtypeStruct((16, ORDER), f32),
            jax.ShapeDtypeStruct((2, TERMS), f32),
        ),
        in_specs=[pl.BlockSpec(memory_space=pl.ANY), vmem, vmem, vmem],
        out_specs=(vmem, vmem, vmem),
        scratch_shapes=[
            pltpu.VMEM((2 * DEPTH, ORDER), jnp.bfloat16),
            pltpu.VMEM((2, 256, 3 * DEPTH), jnp.bfloat16),
            pltpu.VMEM((4, 4, 4, 256, 128), f32),
            pltpu.VMEM((4, 4, 4, 256, 128), f32),
            pltpu.VMEM((4, 4, 4, 256, 128), f32),
            pltpu.VMEM((3, 4, 4, 256, 128), f32),
            pltpu.VMEM((3, 4, 256, 128), f32),
            pltpu.VMEM((3, 256, 128), f32),
            pltpu.VMEM((128, 256), f32),
            pltpu.VMEM((16, 16, 128), f32),
            pltpu.VMEM((8, 16, 256), f32),
            pltpu.VMEM((256, TERMS_PAD), f32),
            pltpu.VMEM((16, 2, TERMS_PAD), f32),
            pltpu.VMEM((8, 2, TERMS_PAD), f32),
            dma((2,)),
            dma((1,)),
            dma((16,)),
            dma((3, 3)),
            dma((3, 32)),
            dma((3, 3)),
            dma((3, 3, 4)),
            dma((3, 3)),
            dma((3, 3)),
            dma((1,)),
            dma((1,)),
            dma((1,)),
            dma((1,)),
            dma((2,)),
            dma((2,)),
        ],
        compiler_params=pltpu.CompilerParams(
            collective_id=0, has_side_effects=True, vmem_limit_bytes=60 * 1024 * 1024
        ),
    )(amplitudes, pauli_x.reshape(1, TERMS), pauli_z.reshape(1, TERMS), pauli_phase.reshape(1, TERMS))


def solution(mesh):
    finer = Mesh(mesh.devices.reshape(mesh.shape["gx"], 2, 2, 4, 2), AXES)
    return jax.shard_map(
        on_device,
        mesh=finer,
        in_specs=(P(None, AXES, None), P(), P(), P()),
        out_specs=(P(AXES, None), P(AXES, None), P()),
        check_vma=False,
    )
```

time: 553 us -> 75.7 us (0.14)
  waiting for transfers between devices: 397 us -> 0 us
  Pallas kernels: 0 us -> 70.5 us
  local copies, waits for them, and re-layouts: 55.7 us -> 4.38 us
  blocking collectives: 31 us -> 0 us
  matrix products: 27.5 us -> 0 us
  other arithmetic: 21.1 us -> 0 us
  between operations: 14.2 us -> 0.64 us
    reduce_scatter x2 -> x0, waiting for transfers between devices: 367 us -> none  [the longest x1 286 us: on_device(): lax.psum_scatter(jnp.concatenate([real_rows, imag_rows], 1), 'gx', scatte...]
    pallas_call x0 -> x1, Pallas kernels: none -> 70.5 us  [on_device(): pl.pallas_call(kernel, out_shape=(jax.ShapeDtypeStruct((16, ORDER), f32),...]
    gather x5 -> x0, local copies, waits for them, and re-layouts: 49.4 us -> none  [the longest x3 24.7 us: on_device(): picked_real = jnp.take_along_axis(density_real, partner, axis=1)]
    psum x5 -> x0, blocking collectives: 31 us -> none  [over_axes(): return functools.reduce(lax.psum, axes, array)]
    all_to_all x1 -> x0, waiting for transfers between devices: 30.2 us -> none  [sent_and_summed(): lax.all_to_all(parts, axis, split_axis=0, concat_axis=0, tiled=True)]
    dot_general x2 -> x0, matrix products: 27.5 us -> none  [the longest x1 14.8 us: on_device(): lax.dot_general(crossed, stacked, dims, preferred_element_type=jnp.float32)]
    concatenate x1 -> x0, other arithmetic: 18.9 us -> none  [on_device(): jnp.concatenate([real_rows, imag_rows], 1)]
  transfers between devices with their start and end apart: 3 -> 0, of which waited for: 3 -> 0; matrix products, arithmetic and copies ran while one was open for 0% -> 0% of each run, Pallas kernels for 0% -> 0%
where the time goes in v2:
time: 75.7 us; the launch traced here: 75.5 us
  Pallas kernels  70.5 us (93%)
  local copies, waits for them, and re-layouts  4.38 us (6%)
    pallas_call x1, Pallas kernels, on_device(): pl.pallas_call(kernel, out_shape=(jax.ShapeDtypeStruct((16, ORDER), f32),...  70.5 us
    unnamed x3, local copies, waits for them, and re-layouts  4.38 us

profile of v2, /device:TPU:1, one launch (start us, length us, event | category | flops | bytes accessed | tf_op | source)
XLA Modules:
  0.0 75.5 jit_solution(4840634891120000881)
XLA Ops:
  0.6 70.5 %shard_map.67 = (f32[16,2048]{1,0:T(8,128)}, f32[16,2048]{1,0:T(8,128)}, f32[2,200]{1,0:T(2,128)}) custom-call(bf16[2,512,2048]{2,1,0:T(8,128)(2,1)} %amp.1, s32[1,200]{1,0:T(1,128)} %bitcast.3, s32[1,200]{1,0:T(1,128)} %bitcast.4, s32[1,200]{1,0:T(1,128)} %bitcast.5), custom_call_target="tpu_custom_call" | custom-call | tf_op jit(solution)/shard_map/pallas_call | solution.py:569
  71.1 1.6 %copy.10 = f32[16,2048]{1,0:T(8,128)} copy(f32[16,2048]{1,0:T(8,128)} %get-tuple-element.6) | data formatting | bytes 262144
  72.7 1.6 %copy.11 = f32[16,2048]{1,0:T(8,128)} copy(f32[16,2048]{1,0:T(8,128)} %get-tuple-element.7) | data formatting | bytes 262144
  74.2 1.2 %copy.12 = f32[2,200]{1,0:T(2,128)} copy(f32[2,200]{1,0:T(2,128)} %get-tuple-element.8) | data formatting | bytes 3200

commit v3 on v2

v3 whole, which is shorter than its diff:
```python
import functools

import jax
import jax.numpy as jnp
from jax import lax
from jax.experimental import pallas as pl
from jax.experimental.pallas import tpu as pltpu
from jax.sharding import Mesh
from jax.sharding import PartitionSpec as P

ORDER = 2048
COLS = 65536
DEPTH = 512
TERMS = 200
TERMS_PAD = 256
AXES = ("gx", "gy_0", "gy_1", "gz_0", "gz_1")
ROWS = (slice(0, 88), slice(88, 176), slice(176, 256))
FAR, PURE, ACC = 0, 1, 2
LAG_Z, LAG_XY = 3, 5
BASE = (0, 8, 16)
TAKE = (0, 4, 8)
UNITS = (
    (2, 2), (2, 3), (3, 2), (2, 1), (1, 2), (3, 3), (3, 1), (1, 3),
    (1, 1), (2, 0), (3, 0), (1, 0), (0, 2), (0, 3), (0, 1), (0, 0),
)
UNITS_Y = tuple(sum(u[0] << 2 * n for n, u in enumerate(UNITS[k : k + 8])) for k in (0, 8))
UNITS_X = tuple(sum(u[1] << 2 * n for n, u in enumerate(UNITS[k : k + 8])) for k in (0, 8))
LO, HI = slice(0, 2), slice(2, 4)
HALF = (LO, HI)


def digit(table, v):
    late = v // 8
    packed = table[0] + late * (table[1] - table[0])
    return (packed >> (2 * (v - 8 * late))) & 3


def remote(src, dst, send, recv, device):
    return pltpu.make_async_remote_copy(
        src_ref=src,
        dst_ref=dst,
        send_sem=send,
        recv_sem=recv,
        device_id=device,
        device_id_type=pl.DeviceIdType.MESH,
    )


def parity(values):
    values = values ^ (values >> 8)
    values = values ^ (values >> 4)
    values = values ^ (values >> 2)
    values = values ^ (values >> 1)
    return values & 1


def kernel(
    amp, px_in, pz_in, pph_in,
    out_re, out_im, out_ex,
    s, t, p, stage, cross, ph1, ph2, ph3, flipped, direct, mirror, weights, pick, part0, part1,
    px, pz, pph, in_sem, core_ss, core_rs, ss1, far1, take_s, ss2, far2, take2_s, ss3, rs3,
    dss, drs, mss, mrs, ess, ers,
):
    x0 = lax.axis_index("gx")
    zh = lax.axis_index("gy_0")
    core = lax.axis_index("gy_1")
    y0 = lax.axis_index("gz_0")
    zl = lax.axis_index("gz_1")
    z0 = 2 * zh + zl
    me = x0 * 32 + zh * 16 + core * 8 + y0 * 2 + zl

    def at_x(step):
        return {"gx": lax.rem(x0 + step, 4)}

    def at_y(step):
        return {"gz_0": lax.rem(y0 + step, 4)}

    def at_z(step):
        z = lax.rem(z0 + step, 4)
        return {"gy_0": z // 2, "gz_1": lax.rem(z, 2)}

    along = (at_x, at_y, at_z)
    along2 = (at_y, at_z, at_x)
    along3 = (at_z, at_x, at_y)
    origin2 = (y0, z0, x0)
    origin3 = (z0, x0, y0)
    other_core = {"gy_1": 1 - core}
    blocks = (4 * (1 - core), 4 * core)

    def transposed(slot, y):
        at = 2 * y + slot
        first = pl.multiple_of((blocks[slot] + y) * 256, 256)
        re_t = s[:DEPTH, pl.ds(first, 256)].T
        im_t = s[DEPTH:, pl.ds(first, 256)].T
        t[at, :, :DEPTH] = re_t
        t[at, :, DEPTH : 2 * DEPTH] = im_t
        t[at, :, 2 * DEPTH :] = -re_t

    def factor(slot, y, imag):
        return t[2 * y + slot, :, pl.ds(pl.multiple_of(imag * DEPTH, DEPTH), 2 * DEPTH)]

    def column(col):
        return s[:, pl.ds(pl.multiple_of(col * 256, 256), 256)]

    dot = functools.partial(jnp.dot, preferred_element_type=jnp.float32)

    def products(y, x):
        for half in range(2):
            col = 2 * x + half
            left = jnp.concatenate(
                [factor(slot, y, (blocks[slot] + y - col + 7) // 8) for slot in range(2)], axis=0
            )
            value = dot(left, column(col))
            for slot, dst in ((0, stage), (1, p)):
                for k in range(2):
                    dst[y, x, 2 * half + k] = value[
                        256 * slot : 256 * slot + 256, 128 * k : 128 * k + 128
                    ]

    def mend(y, x):
        for slot, dst in ((0, stage), (1, p)):
            block = blocks[slot] + y

            @pl.when(block // 2 == x)
            def _(slot=slot, dst=dst, block=block):
                imag = dot(factor(slot, y, 1), column(block))
                row = lax.broadcasted_iota(jnp.int32, (256, 128), 0)
                lane = lax.broadcasted_iota(jnp.int32, (256, 128), 1)
                for k in range(2):
                    z = 2 * lax.rem(block, 2) + k
                    dst[y, x, z] = jnp.where(
                        lane + 128 * k >= row, dst[y, x, z], imag[:, 128 * k : 128 * k + 128]
                    )

    def unit_of(v):
        off_y, off_x = digit(UNITS_Y, v), digit(UNITS_X, v)
        return off_y, off_x, lax.rem(y0 + off_y, 4), lax.rem(x0 + off_x, 4)

    def core_copy(v, y, x):
        return remote(stage.at[y, x], cross.at[y, x], core_ss.at[0], core_rs.at[v], other_core)

    def copy1(kind, o, src, key, index, step):
        line = index // 2 if o < 2 else index
        return remote(
            src,
            ph1.at[(kind,) + key + (ROWS[o],)],
            ss1.at[0],
            far1.at[BASE[o] + index] if kind == FAR else take_s.at[TAKE[o] + line],
            along[o](step),
        )

    def send1(kind, o, src, key, index, step):
        copy1(kind, o, src, key, index, step).start()

    def wait1(o, key, index):
        copy1(FAR, o, ph1.at[(FAR,) + key + (ROWS[o],)], key, index, 1).wait_recv()

    def add_cross(y, x):
        for z in range(4):
            p[y, x, z] += cross[y, x, z]

    def finish(v):
        off_y, off_x, y, x = unit_of(v)
        for o, off, line in ((0, off_x, y), (1, off_y, x)):
            @pl.when(off == 2)
            def _(o=o, line=line):
                for h, step in ((0, 1), (1, 3)):
                    send1(FAR, o, p.at[y, x, HALF[h], ROWS[o]], (line, HALF[h]), 2 * line + h, step)

            @pl.when(off == 1)
            def _(o=o, line=line):
                send1(PURE, o, p.at[y, x, HI, ROWS[o]], (line, HI), 2 * line + 1, 1)

            @pl.when(off == 3)
            def _(o=o, line=line):
                send1(PURE, o, p.at[y, x, LO, ROWS[o]], (line, LO), 2 * line, 3)

        up = lax.rem(v, 2)
        far, right, left = (lax.rem(z0 + k, 4) for k in (2, 1, 3))

        @pl.when(up == 0)
        def _():
            send1(FAR, 2, p.at[y, x, far, ROWS[2]], (y, x), 4 * y + x, 1)
            send1(PURE, 2, p.at[y, x, left, ROWS[2]], (y, x), 4 * y + x, 3)

        @pl.when(up == 1)
        def _():
            send1(FAR, 2, p.at[y, x, far, ROWS[2]], (y, x), 4 * y + x, 3)
            send1(PURE, 2, p.at[y, x, right, ROWS[2]], (y, x), 4 * y + x, 1)

    def forward_xy(v):
        off_y, off_x, y, x = unit_of(v)
        for o, off, line in ((0, off_x, y), (1, off_y, x)):
            for h, step in ((0, 1), (1, 3)):
                @pl.when(off == step)
                def _(o=o, line=line, h=h, step=step):
                    key, index = (line, HALF[h]), 2 * line + h
                    wait1(o, key, index)
                    p[y, x, HALF[h], ROWS[o]] += ph1[FAR, line, HALF[h], ROWS[o]]
                    send1(ACC, o, p.at[y, x, HALF[h], ROWS[o]], key, index, step)

    def forward_z(v):
        _, _, y, x = unit_of(v)
        wait1(2, (y, x), 4 * y + x)
        for h, step in ((0, 1), (1, 3)):
            @pl.when(lax.rem(v, 2) == h)
            def _(step=step):
                z = lax.rem(z0 + step, 4)
                p[y, x, z, ROWS[2]] += ph1[FAR, y, x, ROWS[2]]
                send1(ACC, 2, p.at[y, x, z, ROWS[2]], (y, x), 4 * y + x, step)

    def held(o, b, cs):
        if o == 0:
            return (b, x0, cs, ROWS[0])
        if o == 1:
            return (y0, cs, b, ROWS[1])
        return (cs, b, z0, ROWS[2])

    def landed(o, b, cs):
        return (b, cs, ROWS[0]) if o == 0 else (cs, b, ROWS[o])

    def at2(o, k):
        return lax.rem(origin2[o] + k, 4)

    def at3(o, k):
        return lax.rem(origin3[o] + k, 4)

    groups = ((((LO, 0, 0), (HI, 1, 1)),) + tuple(
        tuple((at3(o, k), n % 2, n) for n, k in enumerate((2, 3, 1, 0))) for o in (1, 2)
    ))

    def arrived(o, line):
        key = (line // 4, lax.rem(line, 4)) if o == 2 else (line, slice(None))
        ref = ph1.at[(slice(PURE, ACC + 1),) + key + (ROWS[o],)]
        remote(ref, ref, ss1.at[0], take_s.at[TAKE[o] + line], other_core).wait_recv()

    def add1(o, b, c):
        p[held(o, b, c)] += ph1[(PURE,) + landed(o, b, c)] + ph1[(ACC,) + landed(o, b, c)]

    def take0(b):
        arrived(0, b)
        for c in range(4):
            add1(0, b, c)

    def copy2(kind, o, src, group, step):
        cs, _, n = group
        return remote(
            src, ph2.at[kind, cs, ROWS[o]], ss2.at[0],
            far2.at[o, n] if kind == FAR else take2_s.at[o, n if o else 0], along2[o](step),
        )

    def wait2(o, group):
        copy2(FAR, o, ph2.at[FAR, group[0], ROWS[o]], group, 1).wait_recv()

    def send2(kind, o, group, step):
        b = at2(o, 2 if kind == FAR else step)
        copy2(kind, o, p.at[held(o, b, group[0])], group, step).start()

    UP = (1, 3)
    DOWN = (3, 1)

    def accumulate2(o, n):
        group = groups[o][n]
        cs, h, _ = group
        wait2(o, group)
        p[held(o, at2(o, UP[h]), cs)] += ph2[FAR, cs, ROWS[o]]
        send2(ACC, o, group, UP[h])

    def far0():
        take0(at2(0, 2))
        for group in groups[0]:
            send2(FAR, 0, group, UP[group[1]])

    def pure0(step):
        take0(at2(0, step))
        for group in groups[0]:
            if DOWN[group[1]] == step:
                send2(PURE, 0, group, step)

    def open2(o, n):
        group = groups[o][n]
        cs, h, _ = group

        def take(k):
            b = at2(o, k)
            if o == 2:
                arrived(2, 4 * cs + b)
            add1(o, b, cs)

        if o == 1:
            arrived(1, cs)
        take(2)
        send2(FAR, o, group, UP[h])
        take(DOWN[h])
        send2(PURE, o, group, DOWN[h])
        take(UP[h])

    def direct2(o):
        c = groups[o][3][0]
        if o == 1:
            arrived(1, c)
        for k in (2, 1, 3):
            b = at2(o, k)
            if o == 2:
                arrived(2, 4 * c + b)
            add1(o, b, c)
            remote(
                p.at[held(o, b, c)], ph2.at[k - 1, c, ROWS[o]],
                ss2.at[0], take2_s.at[o, 3], along2[o](k),
            ).start()

    def own(o, c):
        return held(o, origin2[o], c)

    def send3(o, k):
        remote(
            p.at[own(o, at3(o, k))], ph3.at[k - 1, ROWS[o]], ss3.at[0], rs3.at[o], along3[o](k)
        ).start()

    def close2(o, n):
        c = groups[o][n][0]
        if o == 2:
            arrived(2, 4 * c + x0)
        add1(o, origin2[o], c)
        ref = ph2.at[PURE : ACC + 1, c, ROWS[o]]
        remote(ref, ref, ss2.at[0], take2_s.at[o, n], other_core).wait_recv()
        p[own(o, c)] += ph2[PURE, c, ROWS[o]] + ph2[ACC, c, ROWS[o]]
        send3(o, (2, 3, 1)[n])

    def close0():
        take0(y0)
        ref = ph2.at[PURE : ACC + 1, :, ROWS[0]]
        remote(ref, ref, ss2.at[0], take2_s.at[0, 0], other_core).wait_recv()
        for k in (2, 1, 3, 0):
            c = at3(0, k)
            p[own(0, c)] += ph2[PURE, c, ROWS[0]] + ph2[ACC, c, ROWS[0]]
            if k:
                send3(0, k)

    loads = [
        pltpu.make_async_copy(amp.at[k], s.at[pl.ds(DEPTH * k, DEPTH)], in_sem.at[k])
        for k in range(2)
    ]
    for n, (src, dst) in enumerate(((px_in, px), (pz_in, pz), (pph_in, pph))):
        loads.append(pltpu.make_async_copy(src, dst, in_sem.at[2 + n]))
    for load in loads:
        load.start()
    barrier = pltpu.get_barrier_semaphore()
    partners = [other_core] + [f(k) for f in along for k in (1, 3)]
    for device in partners:
        pl.semaphore_signal(barrier, inc=1, device_id=device, device_id_type=pl.DeviceIdType.MESH)
    for load in loads:
        load.wait()

    for slot in range(2):
        transposed(slot, lax.rem(y0 + 2, 4))
    _, _, y, x = unit_of(0)
    products(y, x)
    mend(y, x)
    pl.semaphore_wait(barrier, len(partners))
    core_copy(0, y, x).start()
    _, _, y, x = unit_of(1)
    products(y, x)
    mend(y, x)
    core_copy(1, y, x).start()

    def settle(v):
        _, _, y, x = unit_of(v)
        core_copy(v, y, x).wait_recv()
        add_cross(y, x)
        finish(v)

    settle(0)
    _, _, y, x = unit_of(2)
    for slot in range(2):
        transposed(slot, y)
    products(y, x)
    mend(y, x)
    core_copy(2, y, x).start()

    def step(u, carry):
        off_y, off_x, y, x = unit_of(u)
        _, _, last_y, last_x = unit_of(u - 2)

        @pl.when(off_x == 2)
        def _():
            for slot in range(2):
                transposed(slot, y)
        core_copy(u - 2, last_y, last_x).wait_recv()
        products(y, x)
        add_cross(last_y, last_x)
        mend(y, x)
        core_copy(u, y, x).start()
        finish(u - 2)

        @pl.when(u >= 2 + LAG_Z)
        def _():
            forward_z(u - 2 - LAG_Z)

        @pl.when(u >= 2 + LAG_XY)
        def _():
            forward_xy(u - 2 - LAG_XY)

        @pl.when(u == 12)
        def _():
            open2(2, 0)

        return carry

    lax.fori_loop(3, 16, step, 0)

    settle(14)
    forward_z(11)
    forward_xy(10)
    accumulate2(2, 0)
    settle(15)
    forward_z(12)
    forward_z(13)
    forward_xy(11)
    far0()
    open2(1, 0)
    open2(2, 1)
    forward_z(14)
    forward_z(15)
    forward_xy(13)
    forward_xy(14)
    row_block = 4 * core + y0
    col_block = 4 * x0 + z0
    xs, zs, phase = px[...], pz[...], pph[...]
    even = parity(xs & zs) == 0
    for n in range(3):
        rows = slice(128 * n, 128 * n + 128)
        pick[rows, :TERMS] = jnp.where(
            lax.broadcasted_iota(jnp.int32, (128, TERMS), 0) == (xs & 127), 1.0, 0.0
        ).astype(jnp.bfloat16)
    count = jnp.where(xs == 0, 1.0, 2.0) * (1.0 / COLS)
    rows = 256 * row_block + lax.broadcasted_iota(jnp.int32, (256, TERMS), 0)
    sign = jnp.where(parity(rows & zs) == 0, count, -count)
    keep = ((rows ^ xs) >> 7) == col_block
    weights[:, :TERMS] = jnp.where(keep & (((rows ^ xs) >= rows) == even), sign, 0.0)

    def phased(share):
        phase_re = jnp.where(phase == 0, 1.0, jnp.where(phase == 2, -1.0, 0.0))
        phase_im = jnp.where(phase == 1, 1.0, jnp.where(phase == 3, -1.0, 0.0))
        return share * jnp.concatenate(
            [jnp.where(even, phase_re, -phase_im), jnp.where(even, phase_im, phase_re)], axis=0
        )
    pure0(3)
    open2(1, 1)
    pure0(1)
    open2(1, 2)
    open2(2, 2)
    accumulate2(1, 0)
    accumulate2(2, 1)
    for n in range(2):
        accumulate2(0, n)
    accumulate2(1, 1)
    direct2(1)
    close2(2, 0)
    accumulate2(1, 2)
    accumulate2(2, 2)
    close2(1, 0)
    close2(2, 1)
    close2(1, 1)
    direct2(2)
    close0()
    close2(1, 2)
    close2(2, 2)

    for o in (1, 2):
        c = origin3[o]
        if o == 2:
            arrived(2, 4 * c + x0)
        add1(o, origin2[o], c)
        ref = ph2.at[:, c, ROWS[o]]
        remote(ref, ref, ss2.at[0], take2_s.at[o, 3], other_core).wait_recv()
        p[own(o, c)] += ph2[0, c, ROWS[o]] + ph2[1, c, ROWS[o]] + ph2[2, c, ROWS[o]]
    for o in range(3):
        ref = ph3.at[:, ROWS[o]]
        remote(ref, ref, ss3.at[0], rs3.at[o], other_core).wait_recv()
    block = p[y0, x0, z0] + ph3[0] + ph3[1] + ph3[2]
    p[y0, x0, z0] = block

    row = lax.broadcasted_iota(jnp.int32, (256, 128), 0)
    lane = lax.broadcasted_iota(jnp.int32, (256, 128), 1)
    moved = block
    for bit in range(7):
        hop = 1 << bit
        swapped = jnp.where(
            (lane & hop) != 0, pltpu.roll(moved, hop, 1), pltpu.roll(moved, 128 - hop, 1)
        )
        moved = jnp.where((row & hop) != 0, swapped, moved)
    high = moved.astype(jnp.bfloat16)
    rest = moved - high.astype(jnp.float32)
    middle = rest.astype(jnp.bfloat16)
    low = (rest - middle.astype(jnp.float32)).astype(jnp.bfloat16)
    read = dot(jnp.concatenate([high, middle, low], axis=1), pick[:, :TERMS])
    here = jnp.sum(weights[:, :TERMS] * read, axis=0, keepdims=True)

    def give(here, parts, n, mine, count, where):
        parts[mine, :, :TERMS] = here
        for k in range(1, count):
            remote(
                parts.at[mine], parts.at[mine], ess.at[n], ers.at[n],
                where(lax.rem(mine + k, count)),
            ).start()

    def collect(parts, n, count):
        rest = parts.at[pl.ds(0, count - 1)]
        remote(rest, rest, ess.at[n], ers.at[n], other_core).wait_recv()
        total = parts[0, :, :TERMS]
        for k in range(1, count):
            total = total + parts[k, :, :TERMS]
        return total

    give(
        here, part0, 0, 4 * x0 + z0, 16,
        lambda k: {"gx": k // 4, "gy_0": lax.rem(k // 2, 2), "gz_1": lax.rem(k, 2)},
    )

    flipped[...] = block.T

    def device(e):
        return {
            "gx": e // 32,
            "gy_0": lax.rem(e // 16, 2),
            "gy_1": lax.rem(e // 8, 2),
            "gz_0": lax.rem(e // 2, 4),
            "gz_1": lax.rem(e, 2),
        }

    def direct_copy(k):
        e = 16 * row_block + k
        return e, remote(
            p.at[y0, x0, z0, pl.ds(16 * k, 16)], direct.at[col_block],
            dss.at[0], drs.at[0], device(e),
        )

    def mirror_copy(k):
        e = 8 * col_block + k
        return e, remote(
            flipped.at[pl.ds(16 * k, 16)], mirror.at[row_block],
            mss.at[0], mrs.at[0], device(e),
        )

    for k in range(16):
        e, copy = direct_copy(k)

        @pl.when(e != me)
        def _(copy=copy):
            copy.start()

        @pl.when(e == me)
        def _(k=k):
            direct[col_block] = p[y0, x0, z0, pl.ds(16 * k, 16)]

    for k in range(8):
        e, copy = mirror_copy(k)

        @pl.when(e != me)
        def _(copy=copy):
            copy.start()

        @pl.when(e == me)
        def _(k=k):
            mirror[row_block] = flipped[pl.ds(16 * k, 16)]

    give(
        collect(part0, 0, 16), part1, 1, 2 * y0 + core, 8,
        lambda k: {"gz_0": k // 2, "gy_1": lax.rem(k, 2)},
    )
    out_ex[...] = phased(collect(part1, 1, 8))

    def landed_and_left(ref, ss, rs):
        copy = remote(ref, ref, ss, rs, other_core)
        copy.wait_recv()
        copy.wait_send()

    @pl.when(me // 16 == row_block)
    def _():
        landed_and_left(direct.at[pl.ds(0, 15)], dss.at[0], drs.at[0])

    @pl.when(me // 16 != row_block)
    def _():
        landed_and_left(direct, dss.at[0], drs.at[0])

    @pl.when(me // 8 == col_block)
    def _():
        landed_and_left(mirror.at[pl.ds(0, 7)], mss.at[0], mrs.at[0])

    @pl.when(me // 8 != col_block)
    def _():
        landed_and_left(mirror, mss.at[0], mrs.at[0])

    row = 16 * me + lax.broadcasted_iota(jnp.int32, (16, 128), 0)
    lane = lax.broadcasted_iota(jnp.int32, (16, 128), 1)
    for k in range(16):
        given = direct[k] * (1.0 / COLS)
        turned = mirror[k // 2, :, 128 * (k % 2) : 128 * (k % 2) + 128] * (1.0 / COLS)
        col = 128 * k + lane
        out_re[:, 128 * k : 128 * k + 128] = jnp.where(col >= row, given, turned)
        out_im[:, 128 * k : 128 * k + 128] = jnp.where(
            col < row, given, jnp.where(col == row, 0.0, -turned)
        )

    def left(ref, sem):
        remote(ref, ref, sem, core_rs.at[0], other_core).wait_send()

    left(stage, core_ss.at[0])
    left(ph1, ss1.at[0])
    left(ph2, ss2.at[0])
    left(ph3, ss3.at[0])
    left(part0.at[pl.ds(0, 15)], ess.at[0])
    left(part1.at[pl.ds(0, 7)], ess.at[1])


def put_out(re, im, ex, out_re, out_im, out_ex):
    out_re[...] = re[...]
    out_im[...] = im[...]
    out_ex[...] = ex[...]


def on_device(amplitudes, pauli_x, pauli_z, pauli_phase):
    vmem = pl.BlockSpec(memory_space=pltpu.VMEM)
    f32 = jnp.float32
    dma = pltpu.SemaphoreType.DMA
    results = pl.pallas_call(
        kernel,
        out_shape=(
            jax.ShapeDtypeStruct((16, ORDER), f32),
            jax.ShapeDtypeStruct((16, ORDER), f32),
            jax.ShapeDtypeStruct((2, TERMS), f32),
        ),
        in_specs=[pl.BlockSpec(memory_space=pltpu.HBM)] * 4,
        out_specs=(vmem, vmem, vmem),
        scratch_shapes=[
            pltpu.VMEM((2 * DEPTH, ORDER), jnp.bfloat16),
            pltpu.VMEM((8, 256, 3 * DEPTH), jnp.bfloat16),
            pltpu.VMEM((4, 4, 4, 256, 128), f32),
            pltpu.VMEM((4, 4, 4, 256, 128), f32),
            pltpu.VMEM((4, 4, 4, 256, 128), f32),
            pltpu.VMEM((3, 4, 4, 256, 128), f32),
            pltpu.VMEM((3, 4, 256, 128), f32),
            pltpu.VMEM((3, 256, 128), f32),
            pltpu.VMEM((128, 256), f32),
            pltpu.VMEM((16, 16, 128), f32),
            pltpu.VMEM((8, 16, 256), f32),
            pltpu.VMEM((256, TERMS_PAD), f32),
            pltpu.VMEM((384, TERMS_PAD), jnp.bfloat16),
            pltpu.VMEM((16, 1, TERMS_PAD), f32),
            pltpu.VMEM((8, 1, TERMS_PAD), f32),
            pltpu.VMEM((1, TERMS), jnp.int32),
            pltpu.VMEM((1, TERMS), jnp.int32),
            pltpu.VMEM((1, TERMS), jnp.int32),
            dma((5,)),
            dma((1,)),
            dma((16,)),
            dma((1,)),
            dma((32,)),
            dma((24,)),
            dma((1,)),
            dma((3, 4)),
            dma((3, 4)),
            dma((1,)),
            dma((3,)),
            dma((1,)),
            dma((1,)),
            dma((1,)),
            dma((1,)),
            dma((2,)),
            dma((2,)),
        ],
        compiler_params=pltpu.CompilerParams(
            collective_id=0, has_side_effects=True, vmem_limit_bytes=45 * 1024 * 1024
        ),
    )(*(pltpu.with_memory_space_constraint(v, pltpu.HBM) for v in (amplitudes, pauli_x.reshape(1, TERMS), pauli_z.reshape(1, TERMS), pauli_phase.reshape(1, TERMS))))
    return pl.pallas_call(
        put_out,
        out_shape=tuple(jax.ShapeDtypeStruct(r.shape, f32) for r in results),
        in_specs=[vmem] * 3,
        out_specs=(vmem,) * 3,
        compiler_params=pltpu.CompilerParams(vmem_limit_bytes=4 * 1024 * 1024),
    )(*results)


def solution(mesh):
    finer = Mesh(mesh.devices.reshape(mesh.shape["gx"], 2, 2, 4, 2), AXES)
    return jax.shard_map(
        on_device,
        mesh=finer,
        in_specs=(P(None, AXES, None), P(), P(), P()),
        out_specs=(P(AXES, None), P(AXES, None), P()),
        check_vma=False,
    )
```

time: 75.7 us -> 61.7 us (0.82)
  Pallas kernels: 70.5 us -> 61 us
  local copies, waits for them, and re-layouts: 4.38 us -> 0 us
    pallas_call x1, Pallas kernels: 70.5 us -> 60.2 us  [on_device(): pl.pallas_call(kernel, out_shape=(jax.ShapeDtypeStruct((16, ORDER), f32),...]
    unnamed x3 -> x0, local copies, waits for them, and re-layouts: 4.38 us -> none
where the time goes in v3:
time: 61.7 us; the launch traced here: 61.6 us
  Pallas kernels  61 us (99%)
  between operations  0.64 us (1%)
    pallas_call x1, Pallas kernels, on_device(): pl.pallas_call(kernel, out_shape=(jax.ShapeDtypeStruct((16, ORDER), f32),...  60.2 us

profile of v3, /device:TPU:1, one launch (start us, length us, event | category | flops | bytes accessed | tf_op | source)
XLA Modules:
  0.0 61.6 jit_solution(13581339967530821054)
XLA Ops:
  0.6 60.2 %shard_map.67 = (f32[16,2048]{1,0:T(8,128)S(1)}, f32[16,2048]{1,0:T(8,128)S(1)}, f32[2,200]{1,0:T(2,128)S(1)}) custom-call(bf16[2,512,2048]{2,1,0:T(8,128)(2,1)} %amp.1, s32[1,200]{1,0:T(1,128)} %bitcast.3, s32[1,200]{1,0:T(1,128)} %bitcast.4, s32[1,200]{1,0:T(1,128)} %bitcast.5), custom_call_target="tpu_custom_call" | custom-call | tf_op jit(solution)/shard_map/pallas_call | solution.py:627
  60.9 0.7 %shard_map.68 = (f32[16,2048]{1,0:T(8,128)}, f32[16,2048]{1,0:T(8,128)}, f32[2,200]{1,0:T(2,128)}) custom-call(f32[16,2048]{1,0:T(8,128)S(1)} %get-tuple-element.6.re, f32[16,2048]{1,0:T(8,128)S(1)} %get-tuple-element.7.im, f32[2,200]{1,0:T(2,128)S(1)} %get-tuple-element.8.ex), custom_call_target="tpu_custom_call" | custom-call | tf_op jit(solution)/shard_map/pallas_call | solution.py:677

commit v4 on v3

--- a/solution.py
+++ b/solution.py
@@ -16,7 +16,7 @@
 AXES = ("gx", "gy_0", "gy_1", "gz_0", "gz_1")
 ROWS = (slice(0, 88), slice(88, 176), slice(176, 256))
 FAR, PURE, ACC = 0, 1, 2
-LAG_Z, LAG_XY = 3, 5
+LAG_Z, LAG_XY = 3, 3
 BASE = (0, 8, 16)
 TAKE = (0, 4, 8)
 UNITS = (
@@ -104,6 +104,12 @@
 
     dot = functools.partial(jnp.dot, preferred_element_type=jnp.float32)
 
+    def half_product(slot, dst, y, x, half):
+        block, col = blocks[slot] + y, 2 * x + half
+        value = dot(factor(slot, y, (block - col + 7) // 8), column(col))
+        for k in range(2):
+            dst[y, x, 2 * half + k] = value[:, 128 * k : 128 * k + 128]
+
     def products(y, x):
         for half in range(2):
             col = 2 * x + half
@@ -117,8 +123,9 @@
                         256 * slot : 256 * slot + 256, 128 * k : 128 * k + 128
                     ]
 
-    def mend(y, x):
-        for slot, dst in ((0, stage), (1, p)):
+    def mend(y, x, slots=(0, 1)):
+        for slot in slots:
+            dst = p if slot else stage
             block = blocks[slot] + y
 
             @pl.when(block // 2 == x)
@@ -138,6 +145,12 @@
 
     def core_copy(v, y, x):
         return remote(stage.at[y, x], cross.at[y, x], core_ss.at[0], core_rs.at[v], other_core)
+
+    def core_half(y, x, half):
+        return remote(
+            stage.at[y, x, HALF[half]], cross.at[y, x, HALF[half]],
+            core_ss.at[0], core_rs.at[16 * half], other_core,
+        )
 
     def copy1(kind, o, src, key, index, step):
         line = index // 2 if o < 2 else index
@@ -352,17 +365,22 @@
     for load in loads:
         load.wait()
 
-    for slot in range(2):
-        transposed(slot, lax.rem(y0 + 2, 4))
     _, _, y, x = unit_of(0)
-    products(y, x)
-    mend(y, x)
+    transposed(0, y)
+    half_product(0, stage, y, x, 0)
+    half_product(0, stage, y, x, 1)
+    mend(y, x, (0,))
     pl.semaphore_wait(barrier, len(partners))
-    core_copy(0, y, x).start()
-    _, _, y, x = unit_of(1)
-    products(y, x)
-    mend(y, x)
-    core_copy(1, y, x).start()
+    for half in range(2):
+        core_half(y, x, half).start()
+    transposed(1, y)
+    half_product(1, p, y, x, 0)
+    half_product(1, p, y, x, 1)
+    mend(y, x, (1,))
+    _, _, next_y, next_x = unit_of(1)
+    products(next_y, next_x)
+    mend(next_y, next_x)
+    core_copy(1, next_y, next_x).start()
 
     def settle(v):
         _, _, y, x = unit_of(v)
@@ -370,7 +388,11 @@
         add_cross(y, x)
         finish(v)
 
-    settle(0)
+    for half in range(2):
+        core_half(y, x, half).wait_recv()
+    for z in range(4):
+        p[y, x, z] += cross[y, x, z]
+    finish(0)
     _, _, y, x = unit_of(2)
     for slot in range(2):
         transposed(slot, y)
@@ -405,25 +427,32 @@
         def _():
             open2(2, 0)
 
+        @pl.when(u == 13)
+        def _():
+            far0()
+
+        @pl.when(u == 15)
+        def _():
+            open2(1, 0)
+            open2(2, 1)
+
         return carry
 
     lax.fori_loop(3, 16, step, 0)
 
     settle(14)
     forward_z(11)
-    forward_xy(10)
-    accumulate2(2, 0)
+    pure0(3)
     settle(15)
     forward_z(12)
+    forward_xy(11)
     forward_z(13)
-    forward_xy(11)
-    far0()
-    open2(1, 0)
-    open2(2, 1)
+    forward_xy(13)
+    accumulate2(2, 0)
+    open2(1, 1)
     forward_z(14)
+    forward_xy(14)
     forward_z(15)
-    forward_xy(13)
-    forward_xy(14)
     row_block = 4 * core + y0
     col_block = 4 * x0 + z0
     xs, zs, phase = px[...], pz[...], pph[...]
@@ -434,10 +463,15 @@
             lax.broadcasted_iota(jnp.int32, (128, TERMS), 0) == (xs & 127), 1.0, 0.0
         ).astype(jnp.bfloat16)
     count = jnp.where(xs == 0, 1.0, 2.0) * (1.0 / COLS)
-    rows = 256 * row_block + lax.broadcasted_iota(jnp.int32, (256, TERMS), 0)
-    sign = jnp.where(parity(rows & zs) == 0, count, -count)
-    keep = ((rows ^ xs) >> 7) == col_block
-    weights[:, :TERMS] = jnp.where(keep & (((rows ^ xs) >= rows) == even), sign, 0.0)
+    row = lax.broadcasted_iota(jnp.int32, (256, TERMS), 0)
+    for c in range(4):
+        cols = jnp.where(row < 88, 4 * x0 + c, jnp.where(row < 176, 4 * c + z0, col_block))
+        rows = 256 * jnp.where(row < 176, row_block, 4 * core + c) + row
+        sign = jnp.where(parity(rows & zs) == 0, count, -count)
+        keep = ((rows ^ xs) >> 7) == cols
+        weights[256 * c : 256 * c + 256, :TERMS] = jnp.where(
+            keep & (((rows ^ xs) >= rows) == even), sign, 0.0
+        )
 
     def phased(share):
         phase_re = jnp.where(phase == 0, 1.0, jnp.where(phase == 2, -1.0, 0.0))
@@ -445,27 +479,25 @@
         return share * jnp.concatenate(
             [jnp.where(even, phase_re, -phase_im), jnp.where(even, phase_im, phase_re)], axis=0
         )
-    pure0(3)
-    open2(1, 1)
     pure0(1)
+    open2(2, 2)
     open2(1, 2)
-    open2(2, 2)
     accumulate2(1, 0)
     accumulate2(2, 1)
-    for n in range(2):
-        accumulate2(0, n)
+    accumulate2(0, 1)
+    accumulate2(0, 0)
     accumulate2(1, 1)
+    close2(2, 0)
+    direct2(2)
     direct2(1)
-    close2(2, 0)
+    close2(1, 0)
+    accumulate2(2, 2)
     accumulate2(1, 2)
-    accumulate2(2, 2)
-    close2(1, 0)
     close2(2, 1)
     close2(1, 1)
-    direct2(2)
     close0()
+    close2(2, 2)
     close2(1, 2)
-    close2(2, 2)
 
     for o in (1, 2):
         c = origin3[o]
@@ -475,21 +507,31 @@
         ref = ph2.at[:, c, ROWS[o]]
         remote(ref, ref, ss2.at[0], take2_s.at[o, 3], other_core).wait_recv()
         p[own(o, c)] += ph2[0, c, ROWS[o]] + ph2[1, c, ROWS[o]] + ph2[2, c, ROWS[o]]
-    for o in range(3):
-        ref = ph3.at[:, ROWS[o]]
-        remote(ref, ref, ss3.at[0], rs3.at[o], other_core).wait_recv()
-    block = p[y0, x0, z0] + ph3[0] + ph3[1] + ph3[2]
-    p[y0, x0, z0] = block
-
-    row = lax.broadcasted_iota(jnp.int32, (256, 128), 0)
-    lane = lax.broadcasted_iota(jnp.int32, (256, 128), 1)
-    moved = block
+
+    moved = jnp.concatenate([p[own(o, c)] for c in range(4) for o in range(3)], axis=0)
+    row = lax.broadcasted_iota(jnp.int32, (1024, 128), 0)
+    lane = lax.broadcasted_iota(jnp.int32, (1024, 128), 1)
     for bit in range(7):
         hop = 1 << bit
-        swapped = jnp.where(
-            (lane & hop) != 0, pltpu.roll(moved, hop, 1), pltpu.roll(moved, 128 - hop, 1)
-        )
-        moved = jnp.where((row & hop) != 0, swapped, moved)
+        if bit < 3:
+            swapped = jnp.where(
+                (lane & hop) != 0, pltpu.roll(moved, hop, 1), pltpu.roll(moved, 128 - hop, 1)
+            )
+            moved = jnp.where((row & hop) != 0, swapped, moved)
+        else:
+            runs = []
+            for first in range(0, 1024, 2 * hop):
+                runs.append(moved[first : first + hop])
+                run = moved[first + hop : first + 2 * hop]
+                if bit < 6:
+                    run = jnp.where(
+                        (lane[:hop] & hop) != 0,
+                        pltpu.roll(run, hop, 1), pltpu.roll(run, 128 - hop, 1),
+                    )
+                else:
+                    run = pltpu.roll(run, hop, 1)
+                runs.append(run)
+            moved = jnp.concatenate(runs, axis=0)
     high = moved.astype(jnp.bfloat16)
     rest = moved - high.astype(jnp.float32)
     middle = rest.astype(jnp.bfloat16)
@@ -517,6 +559,12 @@
         here, part0, 0, 4 * x0 + z0, 16,
         lambda k: {"gx": k // 4, "gy_0": lax.rem(k // 2, 2), "gz_1": lax.rem(k, 2)},
     )
+
+    for o in range(3):
+        ref = ph3.at[:, ROWS[o]]
+        remote(ref, ref, ss3.at[0], rs3.at[o], other_core).wait_recv()
+    block = p[y0, x0, z0] + ph3[0] + ph3[1] + ph3[2]
+    p[y0, x0, z0] = block
 
     flipped[...] = block.T
 
@@ -543,27 +591,35 @@
             mss.at[0], mrs.at[0], device(e),
         )
 
-    for k in range(16):
-        e, copy = direct_copy(k)
-
-        @pl.when(e != me)
-        def _(copy=copy):
-            copy.start()
-
-        @pl.when(e == me)
-        def _(k=k):
-            direct[col_block] = p[y0, x0, z0, pl.ds(16 * k, 16)]
-
-    for k in range(8):
-        e, copy = mirror_copy(k)
-
-        @pl.when(e != me)
-        def _(copy=copy):
-            copy.start()
-
-        @pl.when(e == me)
-        def _(k=k):
-            mirror[row_block] = flipped[pl.ds(16 * k, 16)]
+    @pl.when(me // 16 != row_block)
+    def _():
+        for k in range(16):
+            direct_copy(k)[1].start()
+
+    @pl.when(me // 16 == row_block)
+    def _():
+        for k in range(16):
+            e, copy = direct_copy(k)
+            pl.when(e != me)(copy.start)
+
+            @pl.when(e == me)
+            def _(k=k):
+                direct[col_block] = p[y0, x0, z0, pl.ds(16 * k, 16)]
+
+    @pl.when(me // 8 != col_block)
+    def _():
+        for k in range(8):
+            mirror_copy(k)[1].start()
+
+    @pl.when(me // 8 == col_block)
+    def _():
+        for k in range(8):
+            e, copy = mirror_copy(k)
+            pl.when(e != me)(copy.start)
+
+            @pl.when(e == me)
+            def _(k=k):
+                mirror[row_block] = flipped[pl.ds(16 * k, 16)]
 
     give(
         collect(part0, 0, 16), part1, 1, 2 * y0 + core, 8,
@@ -645,7 +701,7 @@
             pltpu.VMEM((128, 256), f32),
             pltpu.VMEM((16, 16, 128), f32),
             pltpu.VMEM((8, 16, 256), f32),
-            pltpu.VMEM((256, TERMS_PAD), f32),
+            pltpu.VMEM((1024, TERMS_PAD), f32),
             pltpu.VMEM((384, TERMS_PAD), jnp.bfloat16),
             pltpu.VMEM((16, 1, TERMS_PAD), f32),
             pltpu.VMEM((8, 1, TERMS_PAD), f32),
@@ -654,7 +710,7 @@
             pltpu.VMEM((1, TERMS), jnp.int32),
             dma((5,)),
             dma((1,)),
-            dma((16,)),
+            dma((17,)),
             dma((1,)),
             dma((32,)),
             dma((24,)),
@@ -671,7 +727,7 @@
             dma((2,)),
         ],
         compiler_params=pltpu.CompilerParams(
-            collective_id=0, has_side_effects=True, vmem_limit_bytes=45 * 1024 * 1024
+            collective_id=0, has_side_effects=True, vmem_limit_bytes=50 * 1024 * 1024
         ),
     )(*(pltpu.with_memory_space_constraint(v, pltpu.HBM) for v in (amplitudes, pauli_x.reshape(1, TERMS), pauli_z.reshape(1, TERMS), pauli_phase.reshape(1, TERMS))))
     return pl.pallas_call(

time: 61.7 us -> 58.1 us (0.942)
  Pallas kernels: 61 us -> 57.4 us
    pallas_call x1, Pallas kernels: 60.2 us -> 56.7 us  [on_device(): pl.pallas_call(kernel, out_shape=(jax.ShapeDtypeStruct((16, ORDER), f32),...]
where the time goes in v4:
time: 58.1 us; the launch traced here: 58 us
  Pallas kernels  57.4 us (99%)
  between operations  0.64 us (1%)
    pallas_call x1, Pallas kernels, on_device(): pl.pallas_call(kernel, out_shape=(jax.ShapeDtypeStruct((16, ORDER), f32),...  56.7 us

profile of v4, /device:TPU:1, one launch (start us, length us, event | category | flops | bytes accessed | tf_op | source)
XLA Modules:
  0.0 58.0 jit_solution(11130561198476610695)
XLA Ops:
  0.6 56.7 %shard_map.67 = (f32[16,2048]{1,0:T(8,128)S(1)}, f32[16,2048]{1,0:T(8,128)S(1)}, f32[2,200]{1,0:T(2,128)S(1)}) custom-call(bf16[2,512,2048]{2,1,0:T(8,128)(2,1)} %amp.1, s32[1,200]{1,0:T(1,128)} %bitcast.3, s32[1,200]{1,0:T(1,128)} %bitcast.4, s32[1,200]{1,0:T(1,128)} %bitcast.5), custom_call_target="tpu_custom_call" | custom-call | tf_op jit(solution)/shard_map/pallas_call | solution.py:683
  57.3 0.7 %shard_map.68 = (f32[16,2048]{1,0:T(8,128)}, f32[16,2048]{1,0:T(8,128)}, f32[2,200]{1,0:T(2,128)}) custom-call(f32[16,2048]{1,0:T(8,128)S(1)} %get-tuple-element.6.re, f32[16,2048]{1,0:T(8,128)S(1)} %get-tuple-element.7.im, f32[2,200]{1,0:T(2,128)S(1)} %get-tuple-element.8.ex), custom_call_target="tpu_custom_call" | custom-call | tf_op jit(solution)/shard_map/pallas_call | solution.py:733

commit v5 on v4

--- a/solution.py
+++ b/solution.py
@@ -57,7 +57,7 @@
 def kernel(
     amp, px_in, pz_in, pph_in,
     out_re, out_im, out_ex,
-    s, t, p, stage, cross, ph1, ph2, ph3, flipped, direct, mirror, weights, pick, part0, part1,
+    s, t, lower, p, stage, cross, ph1, ph2, ph3, flipped, direct, mirror, weights, pick, shares, part0, part1,
     px, pz, pph, in_sem, core_ss, core_rs, ss1, far1, take_s, ss2, far2, take2_s, ss3, rs3,
     dss, drs, mss, mrs, ess, ers,
 ):
@@ -85,11 +85,14 @@
     origin2 = (y0, z0, x0)
     origin3 = (z0, x0, y0)
     other_core = {"gy_1": 1 - core}
-    blocks = (4 * (1 - core), 4 * core)
+
+    def block_of(slot, y):
+        return 4 * (core + slot - 2 * core * slot) + lax.rem(y + 1, 4)
+
 
     def transposed(slot, y):
         at = 2 * y + slot
-        first = pl.multiple_of((blocks[slot] + y) * 256, 256)
+        first = pl.multiple_of(block_of(slot, y) * 256, 256)
         re_t = s[:DEPTH, pl.ds(first, 256)].T
         im_t = s[DEPTH:, pl.ds(first, 256)].T
         t[at, :, :DEPTH] = re_t
@@ -105,7 +108,7 @@
     dot = functools.partial(jnp.dot, preferred_element_type=jnp.float32)
 
     def half_product(slot, dst, y, x, half):
-        block, col = blocks[slot] + y, 2 * x + half
+        block, col = block_of(slot, y), 2 * x + half
         value = dot(factor(slot, y, (block - col + 7) // 8), column(col))
         for k in range(2):
             dst[y, x, 2 * half + k] = value[:, 128 * k : 128 * k + 128]
@@ -114,7 +117,7 @@
         for half in range(2):
             col = 2 * x + half
             left = jnp.concatenate(
-                [factor(slot, y, (blocks[slot] + y - col + 7) // 8) for slot in range(2)], axis=0
+                [factor(slot, y, (block_of(slot, y) - col + 7) // 8) for slot in range(2)], axis=0
             )
             value = dot(left, column(col))
             for slot, dst in ((0, stage), (1, p)):
@@ -123,21 +126,40 @@
                         256 * slot : 256 * slot + 256, 128 * k : 128 * k + 128
                     ]
 
+    def diagonal(slot, y):
+        block = block_of(slot, y)
+        imag = dot(factor(slot, y, 1), column(block))
+        for k in range(2):
+            lower[k] = imag[:, 128 * k : 128 * k + 128]
+
     def mend(y, x, slots=(0, 1)):
+        row = lax.broadcasted_iota(jnp.int32, (256, 128), 0)
+        lane = lax.broadcasted_iota(jnp.int32, (256, 128), 1)
         for slot in slots:
             dst = p if slot else stage
-            block = blocks[slot] + y
+            block = block_of(slot, y)
 
             @pl.when(block // 2 == x)
-            def _(slot=slot, dst=dst, block=block):
-                imag = dot(factor(slot, y, 1), column(block))
-                row = lax.broadcasted_iota(jnp.int32, (256, 128), 0)
-                lane = lax.broadcasted_iota(jnp.int32, (256, 128), 1)
+            def _(dst=dst, block=block):
                 for k in range(2):
                     z = 2 * lax.rem(block, 2) + k
-                    dst[y, x, z] = jnp.where(
-                        lane + 128 * k >= row, dst[y, x, z], imag[:, 128 * k : 128 * k + 128]
-                    )
+                    dst[y, x, z] = jnp.where(lane + 128 * k >= row, dst[y, x, z], lower[k])
+
+    def unit(y, x, beside=lambda: None):
+        shift = block_of(0, y) // 2 - x
+
+        @pl.when(lax.rem(shift + 4, 2) == 0)
+        def _():
+            products(y, x)
+            diagonal(lax.rem(shift + 4, 4) // 2, y)
+            beside()
+
+        @pl.when(lax.rem(shift + 4, 2) != 0)
+        def _():
+            products(y, x)
+            beside()
+
+        mend(y, x)
 
     def unit_of(v):
         off_y, off_x = digit(UNITS_Y, v), digit(UNITS_X, v)
@@ -308,8 +330,8 @@
         send2(PURE, o, group, DOWN[h])
         take(UP[h])
 
-    def direct2(o):
-        c = groups[o][3][0]
+    def direct2(o, n):
+        c = groups[o][n][0]
         if o == 1:
             arrived(1, c)
         for k in (2, 1, 3):
@@ -319,7 +341,7 @@
             add1(o, b, c)
             remote(
                 p.at[held(o, b, c)], ph2.at[k - 1, c, ROWS[o]],
-                ss2.at[0], take2_s.at[o, 3], along2[o](k),
+                ss2.at[0], take2_s.at[o, n], along2[o](k),
             ).start()
 
     def own(o, c):
@@ -335,9 +357,13 @@
         if o == 2:
             arrived(2, 4 * c + x0)
         add1(o, origin2[o], c)
-        ref = ph2.at[PURE : ACC + 1, c, ROWS[o]]
+        kinds = slice(PURE if n < 2 else FAR, ACC + 1)
+        ref = ph2.at[kinds, c, ROWS[o]]
         remote(ref, ref, ss2.at[0], take2_s.at[o, n], other_core).wait_recv()
-        p[own(o, c)] += ph2[PURE, c, ROWS[o]] + ph2[ACC, c, ROWS[o]]
+        total = ph2[PURE, c, ROWS[o]] + ph2[ACC, c, ROWS[o]]
+        if n == 2:
+            total = total + ph2[FAR, c, ROWS[o]]
+        p[own(o, c)] += total
         send3(o, (2, 3, 1)[n])
 
     def close0():
@@ -350,36 +376,88 @@
             if k:
                 send3(0, k)
 
-    loads = [
-        pltpu.make_async_copy(amp.at[k], s.at[pl.ds(DEPTH * k, DEPTH)], in_sem.at[k])
-        for k in range(2)
+    def share(pieces, first=False):
+        runs = []
+        for o, c in pieces:
+            run = p[own(o, c)]
+            row = ROWS[o].start + lax.broadcasted_iota(jnp.int32, run.shape, 0)
+            lane = lax.broadcasted_iota(jnp.int32, run.shape, 1)
+            runs.append((o, c, run, row, lane))
+        moved = jnp.concatenate([run[2] for run in runs], axis=0)
+        row = jnp.concatenate([run[3] for run in runs], axis=0)
+        lane = jnp.concatenate([run[4] for run in runs], axis=0)
+        for bit in range(7):
+            hop = 1 << bit
+            swapped = jnp.where(
+                (lane & hop) != 0, pltpu.roll(moved, hop, 1), pltpu.roll(moved, 128 - hop, 1)
+            )
+            moved = jnp.where((row & hop) != 0, swapped, moved)
+        high = moved.astype(jnp.bfloat16)
+        rest = moved - high.astype(jnp.float32)
+        middle = rest.astype(jnp.bfloat16)
+        low = (rest - middle.astype(jnp.float32)).astype(jnp.bfloat16)
+        read = dot(jnp.concatenate([high, middle, low], axis=1), pick[:, :TERMS])
+        weight = jnp.concatenate([weights[c, ROWS[o], :TERMS] for o, c in pieces], axis=0)
+        total = jnp.sum(weight * read, axis=0, keepdims=True)
+        shares[:, :TERMS] = total if first else shares[:, :TERMS] + total
+
+    def load(q):
+        columns = pl.ds(pl.multiple_of(512 * q, 512), 512)
+        return [
+            pltpu.make_async_copy(
+                amp.at[k, :, columns], s.at[pl.ds(DEPTH * k, DEPTH), columns], in_sem.at[2 * q + k]
+            )
+            for k in range(2)
+        ]
+
+    def start(q):
+        for copy in load(q):
+            copy.start()
+
+    def loaded(q):
+        for copy in load(q):
+            copy.wait()
+
+    first_y, first_x = lax.rem(y0 + 2, 4), lax.rem(x0 + 2, 4)
+    chunk = block_of(0, first_y) // 2
+    later = [lax.rem(chunk + k, 4) for k in (2, 1, 3)]
+    start(chunk)
+    pl.when(first_x != chunk)(lambda: start(first_x))
+    for q in later:
+        pl.when(first_x != q)(lambda q=q: start(q))
+    terms = [
+        pltpu.make_async_copy(src, dst, in_sem.at[8 + n])
+        for n, (src, dst) in enumerate(((px_in, px), (pz_in, pz), (pph_in, pph)))
     ]
-    for n, (src, dst) in enumerate(((px_in, px), (pz_in, pz), (pph_in, pph))):
-        loads.append(pltpu.make_async_copy(src, dst, in_sem.at[2 + n]))
-    for load in loads:
-        load.start()
+    for copy in terms:
+        copy.start()
     barrier = pltpu.get_barrier_semaphore()
     partners = [other_core] + [f(k) for f in along for k in (1, 3)]
     for device in partners:
         pl.semaphore_signal(barrier, inc=1, device_id=device, device_id_type=pl.DeviceIdType.MESH)
-    for load in loads:
-        load.wait()
+    loaded(chunk)
+    pl.when(first_x != chunk)(lambda: loaded(first_x))
 
     _, _, y, x = unit_of(0)
     transposed(0, y)
     half_product(0, stage, y, x, 0)
     half_product(0, stage, y, x, 1)
+    pl.when(block_of(0, y) // 2 == x)(lambda: diagonal(0, y))
     mend(y, x, (0,))
     pl.semaphore_wait(barrier, len(partners))
     for half in range(2):
         core_half(y, x, half).start()
+    for q in later:
+        pl.when(first_x != q)(lambda q=q: loaded(q))
+    for copy in terms:
+        copy.wait()
     transposed(1, y)
     half_product(1, p, y, x, 0)
     half_product(1, p, y, x, 1)
+    pl.when(block_of(1, y) // 2 == x)(lambda: diagonal(1, y))
     mend(y, x, (1,))
     _, _, next_y, next_x = unit_of(1)
-    products(next_y, next_x)
-    mend(next_y, next_x)
+    unit(next_y, next_x)
     core_copy(1, next_y, next_x).start()
 
     def settle(v):
@@ -396,8 +474,7 @@
     _, _, y, x = unit_of(2)
     for slot in range(2):
         transposed(slot, y)
-    products(y, x)
-    mend(y, x)
+    unit(y, x)
     core_copy(2, y, x).start()
 
     def step(u, carry):
@@ -409,9 +486,7 @@
             for slot in range(2):
                 transposed(slot, y)
         core_copy(u - 2, last_y, last_x).wait_recv()
-        products(y, x)
-        add_cross(last_y, last_x)
-        mend(y, x)
+        unit(y, x, lambda: add_cross(last_y, last_x))
         core_copy(u, y, x).start()
         finish(u - 2)
 
@@ -453,7 +528,7 @@
     forward_z(14)
     forward_xy(14)
     forward_z(15)
-    row_block = 4 * core + y0
+    row_block = block_of(1, y0)
     col_block = 4 * x0 + z0
     xs, zs, phase = px[...], pz[...], pph[...]
     even = parity(xs & zs) == 0
@@ -466,10 +541,10 @@
     row = lax.broadcasted_iota(jnp.int32, (256, TERMS), 0)
     for c in range(4):
         cols = jnp.where(row < 88, 4 * x0 + c, jnp.where(row < 176, 4 * c + z0, col_block))
-        rows = 256 * jnp.where(row < 176, row_block, 4 * core + c) + row
+        rows = 256 * jnp.where(row < 176, row_block, block_of(1, c)) + row
         sign = jnp.where(parity(rows & zs) == 0, count, -count)
         keep = ((rows ^ xs) >> 7) == cols
-        weights[256 * c : 256 * c + 256, :TERMS] = jnp.where(
+        weights[c, :, :TERMS] = jnp.where(
             keep & (((rows ^ xs) >= rows) == even), sign, 0.0
         )
 
@@ -480,25 +555,23 @@
             [jnp.where(even, phase_re, -phase_im), jnp.where(even, phase_im, phase_re)], axis=0
         )
     pure0(1)
-    open2(2, 2)
-    open2(1, 2)
+    direct2(2, 2)
+    direct2(1, 2)
     accumulate2(1, 0)
     accumulate2(2, 1)
     accumulate2(0, 1)
     accumulate2(0, 0)
     accumulate2(1, 1)
     close2(2, 0)
-    direct2(2)
-    direct2(1)
+    direct2(2, 3)
+    direct2(1, 3)
     close2(1, 0)
-    accumulate2(2, 2)
-    accumulate2(1, 2)
     close2(2, 1)
+    close2(2, 2)
     close2(1, 1)
+    close2(1, 2)
+    share([(o, at3(o, k)) for o in (1, 2) for k in (2, 3, 1)], True)
     close0()
-    close2(2, 2)
-    close2(1, 2)
-
     for o in (1, 2):
         c = origin3[o]
         if o == 2:
@@ -508,36 +581,8 @@
         remote(ref, ref, ss2.at[0], take2_s.at[o, 3], other_core).wait_recv()
         p[own(o, c)] += ph2[0, c, ROWS[o]] + ph2[1, c, ROWS[o]] + ph2[2, c, ROWS[o]]
 
-    moved = jnp.concatenate([p[own(o, c)] for c in range(4) for o in range(3)], axis=0)
-    row = lax.broadcasted_iota(jnp.int32, (1024, 128), 0)
-    lane = lax.broadcasted_iota(jnp.int32, (1024, 128), 1)
-    for bit in range(7):
-        hop = 1 << bit
-        if bit < 3:
-            swapped = jnp.where(
-                (lane & hop) != 0, pltpu.roll(moved, hop, 1), pltpu.roll(moved, 128 - hop, 1)
-            )
-            moved = jnp.where((row & hop) != 0, swapped, moved)
-        else:
-            runs = []
-            for first in range(0, 1024, 2 * hop):
-                runs.append(moved[first : first + hop])
-                run = moved[first + hop : first + 2 * hop]
-                if bit < 6:
-                    run = jnp.where(
-                        (lane[:hop] & hop) != 0,
-                        pltpu.roll(run, hop, 1), pltpu.roll(run, 128 - hop, 1),
-                    )
-                else:
-                    run = pltpu.roll(run, hop, 1)
-                runs.append(run)
-            moved = jnp.concatenate(runs, axis=0)
-    high = moved.astype(jnp.bfloat16)
-    rest = moved - high.astype(jnp.float32)
-    middle = rest.astype(jnp.bfloat16)
-    low = (rest - middle.astype(jnp.float32)).astype(jnp.bfloat16)
-    read = dot(jnp.concatenate([high, middle, low], axis=1), pick[:, :TERMS])
-    here = jnp.sum(weights[:, :TERMS] * read, axis=0, keepdims=True)
+    share([(0, c) for c in range(4)] + [(o, at3(o, 0)) for o in (1, 2)])
+    here = shares[:, :TERMS]
 
     def give(here, parts, n, mine, count, where):
         parts[mine, :, :TERMS] = here
@@ -692,6 +737,7 @@
         scratch_shapes=[
             pltpu.VMEM((2 * DEPTH, ORDER), jnp.bfloat16),
             pltpu.VMEM((8, 256, 3 * DEPTH), jnp.bfloat16),
+            pltpu.VMEM((2, 256, 128), f32),
             pltpu.VMEM((4, 4, 4, 256, 128), f32),
             pltpu.VMEM((4, 4, 4, 256, 128), f32),
             pltpu.VMEM((4, 4, 4, 256, 128), f32),
@@ -701,14 +747,15 @@
             pltpu.VMEM((128, 256), f32),
             pltpu.VMEM((16, 16, 128), f32),
             pltpu.VMEM((8, 16, 256), f32),
-            pltpu.VMEM((1024, TERMS_PAD), f32),
+            pltpu.VMEM((4, 256, TERMS_PAD), f32),
             pltpu.VMEM((384, TERMS_PAD), jnp.bfloat16),
+            pltpu.VMEM((1, TERMS_PAD), f32),
             pltpu.VMEM((16, 1, TERMS_PAD), f32),
             pltpu.VMEM((8, 1, TERMS_PAD), f32),
             pltpu.VMEM((1, TERMS), jnp.int32),
             pltpu.VMEM((1, TERMS), jnp.int32),
             pltpu.VMEM((1, TERMS), jnp.int32),
-            dma((5,)),
+            dma((11,)),
             dma((1,)),
             dma((17,)),
             dma((1,)),

time: 58.1 us -> 56.2 us (0.967)
  Pallas kernels: 57.4 us -> 55.4 us
    pallas_call x1, Pallas kernels: 56.7 us -> 54.7 us  [on_device(): pl.pallas_call(kernel, out_shape=(jax.ShapeDtypeStruct((16, ORDER), f32),...]
where the time goes in v5:
time: 56.2 us; the launch traced here: 56.1 us
  Pallas kernels  55.4 us (99%)
  between operations  0.64 us (1%)
    pallas_call x1, Pallas kernels, on_device(): pl.pallas_call(kernel, out_shape=(jax.ShapeDtypeStruct((16, ORDER), f32),...  54.7 us

profile of v5, /device:TPU:1, one launch (start us, length us, event | category | flops | bytes accessed | tf_op | source)
XLA Modules:
  0.0 56.1 jit_solution(2103343151023858198)
XLA Ops:
  0.6 54.7 %shard_map.67 = (f32[16,2048]{1,0:T(8,128)S(1)}, f32[16,2048]{1,0:T(8,128)S(1)}, f32[2,200]{1,0:T(2,128)S(1)}) custom-call(bf16[2,512,2048]{2,1,0:T(8,128)(2,1)} %amp.1, s32[1,200]{1,0:T(1,128)} %bitcast.3, s32[1,200]{1,0:T(1,128)} %bitcast.4, s32[1,200]{1,0:T(1,128)} %bitcast.5), custom_call_target="tpu_custom_call" | custom-call | tf_op jit(solution)/shard_map/pallas_call | solution.py:728
  55.4 0.7 %shard_map.68 = (f32[16,2048]{1,0:T(8,128)}, f32[16,2048]{1,0:T(8,128)}, f32[2,200]{1,0:T(2,128)}) custom-call(f32[16,2048]{1,0:T(8,128)S(1)} %get-tuple-element.6.re, f32[16,2048]{1,0:T(8,128)S(1)} %get-tuple-element.7.im, f32[2,200]{1,0:T(2,128)S(1)} %get-tuple-element.8.ex), custom_call_target="tpu_custom_call" | custom-call | tf_op jit(solution)/shard_map/pallas_call | solution.py:780

commit v6 on v5

--- a/solution.py
+++ b/solution.py
@@ -16,23 +16,15 @@
 AXES = ("gx", "gy_0", "gy_1", "gz_0", "gz_1")
 ROWS = (slice(0, 88), slice(88, 176), slice(176, 256))
 FAR, PURE, ACC = 0, 1, 2
-LAG_Z, LAG_XY = 3, 3
+LAG_Z, LAG_XY = 4, 4
 BASE = (0, 8, 16)
 TAKE = (0, 4, 8)
 UNITS = (
     (2, 2), (2, 3), (3, 2), (2, 1), (1, 2), (3, 3), (3, 1), (1, 3),
     (1, 1), (2, 0), (3, 0), (1, 0), (0, 2), (0, 3), (0, 1), (0, 0),
 )
-UNITS_Y = tuple(sum(u[0] << 2 * n for n, u in enumerate(UNITS[k : k + 8])) for k in (0, 8))
-UNITS_X = tuple(sum(u[1] << 2 * n for n, u in enumerate(UNITS[k : k + 8])) for k in (0, 8))
 LO, HI = slice(0, 2), slice(2, 4)
 HALF = (LO, HI)
-
-
-def digit(table, v):
-    late = v // 8
-    packed = table[0] + late * (table[1] - table[0])
-    return (packed >> (2 * (v - 8 * late))) & 3
 
 
 def remote(src, dst, send, recv, device):
@@ -57,7 +49,7 @@
 def kernel(
     amp, px_in, pz_in, pph_in,
     out_re, out_im, out_ex,
-    s, t, lower, p, stage, cross, ph1, ph2, ph3, flipped, direct, mirror, weights, pick, shares, part0, part1,
+    s, t0, t1, t2, t3, lower, p, stage, cross, ph1, ph2, ph3, flipped, direct, mirror, weights, pick, shares, part0, part1,
     px, pz, pph, in_sem, core_ss, core_rs, ss1, far1, take_s, ss2, far2, take2_s, ss3, rs3,
     dss, drs, mss, mrs, ess, ers,
 ):
@@ -90,34 +82,45 @@
         return 4 * (core + slot - 2 * core * slot) + lax.rem(y + 1, 4)
 
 
-    def transposed(slot, y):
-        at = 2 * y + slot
-        first = pl.multiple_of(block_of(slot, y) * 256, 256)
+    flips = (t0, t1, t2, t3)
+
+    def at_offset(off_y):
+        return lax.rem(y0 + off_y, 4)
+
+    def transposed(slot, off_y):
+        t = flips[off_y]
+        first = pl.multiple_of(block_of(slot, at_offset(off_y)) * 256, 256)
         re_t = s[:DEPTH, pl.ds(first, 256)].T
         im_t = s[DEPTH:, pl.ds(first, 256)].T
-        t[at, :, :DEPTH] = re_t
-        t[at, :, DEPTH : 2 * DEPTH] = im_t
-        t[at, :, 2 * DEPTH :] = -re_t
-
-    def factor(slot, y, imag):
-        return t[2 * y + slot, :, pl.ds(pl.multiple_of(imag * DEPTH, DEPTH), 2 * DEPTH)]
+        t[slot, :, :DEPTH] = re_t
+        t[slot, :, DEPTH : 2 * DEPTH] = im_t
+        t[slot, :, 2 * DEPTH :] = -re_t
+
+    def factor(slot, off_y, imag):
+        return flips[off_y][slot, :, pl.ds(pl.multiple_of(imag * DEPTH, DEPTH), 2 * DEPTH)]
 
     def column(col):
         return s[:, pl.ds(pl.multiple_of(col * 256, 256), 256)]
 
     dot = functools.partial(jnp.dot, preferred_element_type=jnp.float32)
 
-    def half_product(slot, dst, y, x, half):
+    def half_product(slot, dst, off_y, x, half):
+        y = at_offset(off_y)
         block, col = block_of(slot, y), 2 * x + half
-        value = dot(factor(slot, y, (block - col + 7) // 8), column(col))
+        value = dot(factor(slot, off_y, (block - col + 7) // 8), column(col))
         for k in range(2):
             dst[y, x, 2 * half + k] = value[:, 128 * k : 128 * k + 128]
 
-    def products(y, x):
+    def products(off_y, x):
+        y = at_offset(off_y)
         for half in range(2):
             col = 2 * x + half
             left = jnp.concatenate(
-                [factor(slot, y, (block_of(slot, y) - col + 7) // 8) for slot in range(2)], axis=0
+                [
+                    factor(slot, off_y, (block_of(slot, y) - col + 7) // 8)
+                    for slot in range(2)
+                ],
+                axis=0,
             )
             value = dot(left, column(col))
             for slot, dst in ((0, stage), (1, p)):
@@ -126,9 +129,8 @@
                         256 * slot : 256 * slot + 256, 128 * k : 128 * k + 128
                     ]
 
-    def diagonal(slot, y):
-        block = block_of(slot, y)
-        imag = dot(factor(slot, y, 1), column(block))
+    def diagonal(slot, off_y):
+        imag = dot(factor(slot, off_y, 1), column(block_of(slot, at_offset(off_y))))
         for k in range(2):
             lower[k] = imag[:, 128 * k : 128 * k + 128]
 
@@ -145,24 +147,27 @@
                     z = 2 * lax.rem(block, 2) + k
                     dst[y, x, z] = jnp.where(lane + 128 * k >= row, dst[y, x, z], lower[k])
 
-    def unit(y, x, beside=lambda: None):
+    def unit(v, beside=lambda: None):
+        off_y, _, y, x = unit_of(v)
         shift = block_of(0, y) // 2 - x
 
         @pl.when(lax.rem(shift + 4, 2) == 0)
         def _():
-            products(y, x)
-            diagonal(lax.rem(shift + 4, 4) // 2, y)
+            products(off_y, x)
+            diagonal(lax.rem(shift + 4, 4) // 2, off_y)
             beside()
 
         @pl.when(lax.rem(shift + 4, 2) != 0)
         def _():
-            products(y, x)
+            products(off_y, x)
             beside()
 
         mend(y, x)
+        if v:
+            core_copy(v, y, x).start()
 
     def unit_of(v):
-        off_y, off_x = digit(UNITS_Y, v), digit(UNITS_X, v)
+        off_y, off_x = UNITS[v]
         return off_y, off_x, lax.rem(y0 + off_y, 4), lax.rem(x0 + off_x, 4)
 
     def core_copy(v, y, x):
@@ -210,7 +215,7 @@
             def _(o=o, line=line):
                 send1(PURE, o, p.at[y, x, LO, ROWS[o]], (line, LO), 2 * line, 3)
 
-        up = lax.rem(v, 2)
+        up = v % 2
         far, right, left = (lax.rem(z0 + k, 4) for k in (2, 1, 3))
 
         @pl.when(up == 0)
@@ -238,7 +243,7 @@
         _, _, y, x = unit_of(v)
         wait1(2, (y, x), 4 * y + x)
         for h, step in ((0, 1), (1, 3)):
-            @pl.when(lax.rem(v, 2) == h)
+            @pl.when(v % 2 == h)
             def _(step=step):
                 z = lax.rem(z0 + step, 4)
                 p[y, x, z, ROWS[2]] += ph1[FAR, y, x, ROWS[2]]
@@ -439,10 +444,10 @@
     pl.when(first_x != chunk)(lambda: loaded(first_x))
 
     _, _, y, x = unit_of(0)
-    transposed(0, y)
-    half_product(0, stage, y, x, 0)
-    half_product(0, stage, y, x, 1)
-    pl.when(block_of(0, y) // 2 == x)(lambda: diagonal(0, y))
+    transposed(0, 2)
+    half_product(0, stage, 2, x, 0)
+    half_product(0, stage, 2, x, 1)
+    pl.when(block_of(0, y) // 2 == x)(lambda: diagonal(0, 2))
     mend(y, x, (0,))
     pl.semaphore_wait(barrier, len(partners))
     for half in range(2):
@@ -451,14 +456,17 @@
         pl.when(first_x != q)(lambda q=q: loaded(q))
     for copy in terms:
         copy.wait()
-    transposed(1, y)
-    half_product(1, p, y, x, 0)
-    half_product(1, p, y, x, 1)
-    pl.when(block_of(1, y) // 2 == x)(lambda: diagonal(1, y))
+    transposed(1, 2)
+    half_product(1, p, 2, x, 0)
+    half_product(1, p, 2, x, 1)
+    pl.when(block_of(1, y) // 2 == x)(lambda: diagonal(1, 2))
     mend(y, x, (1,))
-    _, _, next_y, next_x = unit_of(1)
-    unit(next_y, next_x)
-    core_copy(1, next_y, next_x).start()
+
+    def turned(off_y):
+        for slot in range(2):
+            transposed(slot, off_y)
+
+    unit(1, lambda: turned(3))
 
     def settle(v):
         _, _, y, x = unit_of(v)
@@ -468,62 +476,43 @@
 
     for half in range(2):
         core_half(y, x, half).wait_recv()
-    for z in range(4):
-        p[y, x, z] += cross[y, x, z]
+    add_cross(y, x)
     finish(0)
-    _, _, y, x = unit_of(2)
-    for slot in range(2):
-        transposed(slot, y)
-    unit(y, x)
-    core_copy(2, y, x).start()
-
-    def step(u, carry):
-        off_y, off_x, y, x = unit_of(u)
+    unit(2)
+
+    for u in range(3, 16):
         _, _, last_y, last_x = unit_of(u - 2)
-
-        @pl.when(off_x == 2)
-        def _():
-            for slot in range(2):
-                transposed(slot, y)
         core_copy(u - 2, last_y, last_x).wait_recv()
-        unit(y, x, lambda: add_cross(last_y, last_x))
-        core_copy(u, y, x).start()
+
+        def beside(u=u, last_y=last_y, last_x=last_x):
+            add_cross(last_y, last_x)
+            if u in (3, 7):
+                turned(1 if u == 3 else 0)
+
+        unit(u, beside)
         finish(u - 2)
-
-        @pl.when(u >= 2 + LAG_Z)
-        def _():
+        if u >= 2 + LAG_Z:
             forward_z(u - 2 - LAG_Z)
-
-        @pl.when(u >= 2 + LAG_XY)
-        def _():
+        if u >= 2 + LAG_XY:
             forward_xy(u - 2 - LAG_XY)
-
-        @pl.when(u == 12)
-        def _():
+        if u == 13:
             open2(2, 0)
-
-        @pl.when(u == 13)
-        def _():
+        if u == 14:
             far0()
 
-        @pl.when(u == 15)
-        def _():
-            open2(1, 0)
-            open2(2, 1)
-
-        return carry
-
-    lax.fori_loop(3, 16, step, 0)
-
     settle(14)
+    forward_z(10)
+    forward_xy(10)
+    settle(15)
     forward_z(11)
+    forward_xy(11)
+    forward_z(12)
     pure0(3)
-    settle(15)
-    forward_z(12)
-    forward_xy(11)
+    open2(1, 0)
     forward_z(13)
     forward_xy(13)
     accumulate2(2, 0)
+    open2(2, 1)
     open2(1, 1)
     forward_z(14)
     forward_xy(14)
@@ -565,8 +554,8 @@
     close2(2, 0)
     direct2(2, 3)
     direct2(1, 3)
+    close2(2, 1)
     close2(1, 0)
-    close2(2, 1)
     close2(2, 2)
     close2(1, 1)
     close2(1, 2)
@@ -636,9 +625,13 @@
             mss.at[0], mrs.at[0], device(e),
         )
 
+    far_first = [
+        8 * half + 2 * lax.rem(y0 + k, 4) + low
+        for half in range(2) for k in (2, 3, 1, 0) for low in range(2)
+    ]
     @pl.when(me // 16 != row_block)
     def _():
-        for k in range(16):
+        for k in far_first:
             direct_copy(k)[1].start()
 
     @pl.when(me // 16 == row_block)
@@ -653,7 +646,7 @@
 
     @pl.when(me // 8 != col_block)
     def _():
-        for k in range(8):
+        for k in far_first[:8]:
             mirror_copy(k)[1].start()
 
     @pl.when(me // 8 == col_block)
@@ -736,7 +729,7 @@
         out_specs=(vmem, vmem, vmem),
         scratch_shapes=[
             pltpu.VMEM((2 * DEPTH, ORDER), jnp.bfloat16),
-            pltpu.VMEM((8, 256, 3 * DEPTH), jnp.bfloat16),
+            *[pltpu.VMEM((2, 256, 3 * DEPTH), jnp.bfloat16)] * 4,
             pltpu.VMEM((2, 256, 128), f32),
             pltpu.VMEM((4, 4, 4, 256, 128), f32),
             pltpu.VMEM((4, 4, 4, 256, 128), f32),

time: 56.2 us -> 55.5 us (0.988)
  Pallas kernels: 55.4 us -> 54.7 us
    pallas_call x1, Pallas kernels: 54.7 us -> 54 us  [on_device(): pl.pallas_call(kernel, out_shape=(jax.ShapeDtypeStruct((16, ORDER), f32),...]
where the time goes in v6:
time: 55.5 us; the launch traced here: 55.4 us
  Pallas kernels  54.7 us (99%)
  between operations  0.64 us (1%)
    pallas_call x1, Pallas kernels, on_device(): pl.pallas_call(kernel, out_shape=(jax.ShapeDtypeStruct((16, ORDER), f32),...  54 us

profile of v6, /device:TPU:1, one launch (start us, length us, event | category | flops | bytes accessed | tf_op | source)
XLA Modules:
  0.0 55.4 jit_solution(2509360076604968372)
XLA Ops:
  0.6 54.0 %shard_map.67 = (f32[16,2048]{1,0:T(8,128)S(1)}, f32[16,2048]{1,0:T(8,128)S(1)}, f32[2,200]{1,0:T(2,128)S(1)}) custom-call(bf16[2,512,2048]{2,1,0:T(8,128)(2,1)} %amp.1, s32[1,200]{1,0:T(1,128)} %bitcast.3, s32[1,200]{1,0:T(1,128)} %bitcast.4, s32[1,200]{1,0:T(1,128)} %bitcast.5), custom_call_target="tpu_custom_call" | custom-call | tf_op jit(solution)/shard_map/pallas_call | solution.py:721
  54.7 0.7 %shard_map.68 = (f32[16,2048]{1,0:T(8,128)}, f32[16,2048]{1,0:T(8,128)}, f32[2,200]{1,0:T(2,128)}) custom-call(f32[16,2048]{1,0:T(8,128)S(1)} %get-tuple-element.6.re, f32[16,2048]{1,0:T(8,128)S(1)} %get-tuple-element.7.im, f32[2,200]{1,0:T(2,128)S(1)} %get-tuple-element.8.ex), custom_call_target="tpu_custom_call" | custom-call | tf_op jit(solution)/shard_map/pallas_call | solution.py:773

commit v7 on v6

--- a/solution.py
+++ b/solution.py
@@ -503,20 +503,6 @@
     settle(14)
     forward_z(10)
     forward_xy(10)
-    settle(15)
-    forward_z(11)
-    forward_xy(11)
-    forward_z(12)
-    pure0(3)
-    open2(1, 0)
-    forward_z(13)
-    forward_xy(13)
-    accumulate2(2, 0)
-    open2(2, 1)
-    open2(1, 1)
-    forward_z(14)
-    forward_xy(14)
-    forward_z(15)
     row_block = block_of(1, y0)
     col_block = 4 * x0 + z0
     xs, zs, phase = px[...], pz[...], pph[...]
@@ -543,6 +529,20 @@
         return share * jnp.concatenate(
             [jnp.where(even, phase_re, -phase_im), jnp.where(even, phase_im, phase_re)], axis=0
         )
+    settle(15)
+    forward_z(11)
+    forward_xy(11)
+    forward_z(12)
+    pure0(3)
+    open2(1, 0)
+    forward_z(13)
+    forward_xy(13)
+    accumulate2(2, 0)
+    open2(2, 1)
+    open2(1, 1)
+    forward_z(14)
+    forward_xy(14)
+    forward_z(15)
     pure0(1)
     direct2(2, 2)
     direct2(1, 2)
@@ -590,8 +590,7 @@
         return total
 
     give(
-        here, part0, 0, 4 * x0 + z0, 16,
-        lambda k: {"gx": k // 4, "gy_0": lax.rem(k // 2, 2), "gz_1": lax.rem(k, 2)},
+        here, part1, 1, 2 * y0 + core, 8, lambda k: {"gz_0": k // 2, "gy_1": lax.rem(k, 2)}
     )
 
     for o in range(3):
@@ -600,7 +599,6 @@
     block = p[y0, x0, z0] + ph3[0] + ph3[1] + ph3[2]
     p[y0, x0, z0] = block
 
-    flipped[...] = block.T
 
     def device(e):
         return {
@@ -644,6 +642,13 @@
             def _(k=k):
                 direct[col_block] = p[y0, x0, z0, pl.ds(16 * k, 16)]
 
+
+    give(
+        collect(part1, 1, 8), part0, 0, 4 * x0 + z0, 16,
+        lambda k: {"gx": k // 4, "gy_0": lax.rem(k // 2, 2), "gz_1": lax.rem(k, 2)},
+    )
+    flipped[...] = block.T
+
     @pl.when(me // 8 != col_block)
     def _():
         for k in far_first[:8]:
@@ -658,12 +663,7 @@
             @pl.when(e == me)
             def _(k=k):
                 mirror[row_block] = flipped[pl.ds(16 * k, 16)]
-
-    give(
-        collect(part0, 0, 16), part1, 1, 2 * y0 + core, 8,
-        lambda k: {"gz_0": k // 2, "gy_1": lax.rem(k, 2)},
-    )
-    out_ex[...] = phased(collect(part1, 1, 8))
+    out_ex[...] = phased(collect(part0, 0, 16))
 
     def landed_and_left(ref, ss, rs):
         copy = remote(ref, ref, ss, rs, other_core)

time: 55.5 us -> 55.9 us (level)
  no operation moved by 1% of the time
where the time goes in v7:
time: 55.9 us; the launch traced here: 55.8 us
  Pallas kernels  55.2 us (99%)
  between operations  0.64 us (1%)
    pallas_call x1, Pallas kernels, on_device(): pl.pallas_call(kernel, out_shape=(jax.ShapeDtypeStruct((16, ORDER), f32),...  54.5 us

profile of v7, /device:TPU:1, one launch (start us, length us, event | category | flops | bytes accessed | tf_op | source)
XLA Modules:
  0.0 55.8 jit_solution(13556312409606235129)
XLA Ops:
  0.6 54.5 %shard_map.67 = (f32[16,2048]{1,0:T(8,128)S(1)}, f32[16,2048]{1,0:T(8,128)S(1)}, f32[2,200]{1,0:T(2,128)S(1)}) custom-call(bf16[2,512,2048]{2,1,0:T(8,128)(2,1)} %amp.1, s32[1,200]{1,0:T(1,128)} %bitcast.3, s32[1,200]{1,0:T(1,128)} %bitcast.4, s32[1,200]{1,0:T(1,128)} %bitcast.5), custom_call_target="tpu_custom_call" | custom-call | tf_op jit(solution)/shard_map/pallas_call | solution.py:721
  55.1 0.7 %shard_map.68 = (f32[16,2048]{1,0:T(8,128)}, f32[16,2048]{1,0:T(8,128)}, f32[2,200]{1,0:T(2,128)}) custom-call(f32[16,2048]{1,0:T(8,128)S(1)} %get-tuple-element.6.re, f32[16,2048]{1,0:T(8,128)S(1)} %get-tuple-element.7.im, f32[2,200]{1,0:T(2,128)S(1)} %get-tuple-element.8.ex), custom_call_target="tpu_custom_call" | custom-call | tf_op jit(solution)/shard_map/pallas_call | solution.py:773
